TPU v7x, 512 devices: a whole 4x8x8 slice. The times are simulated.
512 devices in a mesh: gx: 8 (over y), gy: 8 (over x, core), gz: 8 (over z).
Axes of the slice: x: 4, y: 8, z: 8, core: 2. Of those that a mesh axis runs over, the one named last changes fastest.
Arguments:
- wavefunctions: bfloat16 [128, 128, 128, 128], P('gx', 'gy', 'gz'), may hold values from -512 to 512, as said below
- potential: float32 [128, 128, 128], P('gx', 'gy', 'gz'), may hold values from 0 to 3
Outputs:
- rotated: float32 [128, 128, 128, 128], P('gx', 'gy', 'gz')
- residual: bfloat16 [128, 128, 128, 128], P('gx', 'gy', 'gz')
- quotients: float32 [128], replicated
- norms: float32 [128], replicated
Inputs may be any that keep to these rules, and one draw needn't show every extreme that they name: `wavefunctions`: real values mixed across bands, of full rank.
All inputs are finite; a program needn't handle non-finite values.
Results may differ from a plain program's by a relative error of at most 0.0007.
Values may be sent and summed in bfloat16 or wider, within the bound.
No kernel may reach another device: no remote copies, remote signals or barrier semaphores. Data moves between devices by JAX's collectives and lax.ppermute only.
A program may use at most 64 MiB of HBM per device.

v0:
```python
import functools

import jax
import jax.numpy as jnp
from jax import lax
from jax.sharding import Mesh
from jax.sharding import PartitionSpec as P

GY = ("gy_0", "gy_1")
GX_GY_GZ = ("gx", "gy_0", "gy_1", "gz")


def split_up(value, dim, count):
    dims = value.shape
    blocks = value.reshape(*dims[:dim], count, dims[dim] // count, *dims[dim + 1 :])
    return jnp.moveaxis(blocks, dim, 0)


def sum_at_owner(value, axis, dim):
    count = lax.axis_size(axis)
    blocks = lax.all_to_all(split_up(value, dim, count), axis, 0, 0, tiled=True)
    return jnp.sum(blocks, axis=0)


def sum_in_two_steps(value, axes, dim):
    far, near = axes
    own = sum_at_owner(split_up(value, dim, lax.axis_size(far)), near, dim + 1)
    return jnp.sum(lax.all_to_all(own, far, 0, 0, tiled=True), axis=0)


def rows_for(lines, count):
    spare = -lines.shape[0] % count
    if not spare:
        return lines
    return jnp.concatenate([lines, jnp.zeros((spare, *lines.shape[1:]), lines.dtype)])


def copy_for_each(value, axis):
    copies = jnp.broadcast_to(value, (lax.axis_size(axis), *value.shape))
    return lax.all_to_all(copies, axis, split_axis=0, concat_axis=0, tiled=True)


def laid_out(blocks, dim):
    dims = list(blocks.shape[1:])
    dims[dim] *= blocks.shape[0]
    return jnp.moveaxis(blocks, 0, dim).reshape(dims)


def whole_of(value, axes, dim):
    far, near = axes
    initial = copy_for_each(value, far)
    blocks = jnp.swapaxes(copy_for_each(initial, near), 0, 1)
    return laid_out(blocks.reshape(-1, *value.shape), dim)


def sum_by_parts(value, axes):
    lines = value.reshape(-1)
    own = sum_in_two_steps(
        rows_for(lines, lax.axis_size(axes[0]) * lax.axis_size(axes[1])), axes, 0
    )
    whole = whole_of(own, axes, 0)
    return whole[: len(lines)].reshape(value.shape)


def padded_2(value, sides, width):
    edges = {}
    for axis, dim in sides:
        count, length = (lax.axis_size(axis), value.shape[dim])
        up = [(i, (i + 1) % count) for i in range(count)]
        last = lax.slice_in_dim(value, length - width, length, axis=dim)
        initial = lax.slice_in_dim(value, 0, width, axis=dim)
        edges[dim] = (
            lax.ppermute(last, axis, up),
            lax.ppermute(initial, axis, [(b, a) for a, b in up]),
        )
    done = []
    for _, dim in sides:
        low, high = edges[dim]
        around = [(width, width) if d in done else (0, 0) for d in range(value.ndim)]
        value = jnp.concatenate([jnp.pad(low, around), value, jnp.pad(high, around)], axis=dim)
        done.append(dim)
    return value


def by_axis(value, axes):
    return functools.reduce(lax.psum, axes, value)


def stencil(padded, center, potential):
    cx, cy, cz = (center.shape[0], center.shape[1], center.shape[2])
    total = -30.0 * 3.0 * center
    weights = ((0, -1.0), (1, 16.0), (3, 16.0), (4, -1.0))
    for offset, weight in weights:
        total = total + weight * padded[offset : offset + cx, 2 : 2 + cy, 2 : 2 + cz]
        total = total + weight * padded[2 : 2 + cx, offset : offset + cy, 2 : 2 + cz]
        total = total + weight * padded[2 : 2 + cx, 2 : 2 + cy, offset : offset + cz]
    return -0.5 * total / 12.0 + potential[..., None] * center


def rotate(field, inverse):
    shape = field.shape
    flat = field.reshape(-1, shape[3])
    return jnp.dot(flat, inverse.T, precision=lax.Precision.HIGHEST).reshape(shape)


def local(wavefunctions, potential):
    cx, cy, cz, bands = wavefunctions.shape
    total_cells = cx * cy * cz * lax.axis_size("gx") * lax.axis_size(GY) * lax.axis_size("gz")
    flat = wavefunctions.reshape(-1, bands)
    local_correlation = lax.dot_general(
        flat, flat, (((0,), (0,)), ((), ())), preferred_element_type=jnp.float32
    )
    correlation = sum_by_parts(local_correlation, (("gx", "gy_0"), ("gy_1", "gz"))) / total_cells
    factor = jnp.linalg.cholesky(correlation)
    inverse = lax.linalg.triangular_solve(
        factor, jnp.eye(bands, dtype=jnp.float32), left_side=True, lower=True
    )
    given = wavefunctions.astype(jnp.float32)
    raw_padded = padded_2(wavefunctions, (("gx", 0), (GY, 1), ("gz", 2)), 2)
    raw_applied = stencil(raw_padded.astype(jnp.float32), given, potential)
    rotated = rotate(given, inverse)
    applied = rotate(raw_applied, inverse)
    cross = jnp.sum(rotated * applied, axis=(0, 1, 2))
    self_applied = jnp.sum(applied * applied, axis=(0, 1, 2))
    self_rotated = jnp.sum(rotated * rotated, axis=(0, 1, 2))
    cross_all, applied_all, rotated_all = (
        by_axis(cross, GX_GY_GZ),
        by_axis(self_applied, GX_GY_GZ),
        by_axis(self_rotated, GX_GY_GZ),
    )
    quotients = cross_all / total_cells
    squares = applied_all - 2.0 * quotients * cross_all + quotients * quotients * rotated_all
    leftover = applied - quotients * rotated
    norms = jnp.sqrt(squares / total_cells + 1e-06)
    return (rotated, leftover.astype(jnp.bfloat16), quotients, norms)


def solution(mesh):
    torus = Mesh(
        mesh.devices.reshape(mesh.shape["gx"], 4, 2, mesh.shape["gz"]), ("gx", "gy_0", "gy_1", "gz")
    )
    return jax.shard_map(
        local,
        mesh=torus,
        in_specs=(P("gx", GY, "gz", None), P("gx", GY, "gz")),
        out_specs=(P("gx", GY, "gz", None), P("gx", GY, "gz", None), P(), P()),
        check_vma=False,
    )
```

profile of v0, /device:TPU:1, one launch (start us, length us, event | category | flops | bytes accessed | tf_op | source)
XLA Modules:
  0.0 169.2 jit_solution(17151246785656259659)
XLA Ops:
  0.6 2.1 %convolution_bitcast_fusion.1 = f32[128,128]{1,0:T(8,128)S(1)} fusion(bf16[16,16,16,128]{3,2,1,0:T(8,128)(2,1)} %param.2), kind=kOutput, calls=%fused_computation.55 | convolution fusion | flops 134217728 | bytes 1114112 | tf_op jit(solution)/shard_map/dot_general | solution.py:110
  3.0 0.8 reshape.42
  3.8 11.8 %all-to-all-start = ((f32[16,1,1024]{2,1,0:T(1,128)}), f32[16,1,1024]{2,1,0:T(1,128)S(1)}, u32[]{:S(2)}, u32[]{:S(2)}) async-start(f32[16,1,1024]{2,1,0:T(1,128)} %reshape.42), calls=%async_computation | async-start | bytes 131072 | tf_op jit(solution)/shard_map/all_to_all | solution.py:21
  15.6 1.2 collective-permute-start.1
  16.8 0.2 fusion.48
  17.1 3.5 %collective-permute-start = (bf16[16,16,2,128]{3,2,1,0:T(2,128)(2,1)S(1)}, bf16[16,16,2,128]{3,2,1,0:T(2,128)(2,1)S(1)}, u32[]{:S(2)}, u32[]{:S(2)}) collective-permute-start(bf16[16,16,2,128]{3,2,1,0:T(2,128)(2,1)S(1)} %get-tuple-element.26), channel_id=1, source_target_pairs={{0,1},{1,2},{2,3},{3,4},{4,5},{5,6},{6,7},{7,0},{8,9},{9,10},{10,1... | collective-permute-start | bytes 393224 | tf_op jit(solution)/shard_map/ppermute | solution.py:73
  20.6 3.1 %collective-permute-start.5 = (bf16[16,16,2,128]{3,2,1,0:T(2,128)(2,1)S(1)}, bf16[16,16,2,128]{3,2,1,0:T(2,128)(2,1)S(1)}, u32[]{:S(2)}, u32[]{:S(2)}) collective-permute-start(bf16[16,16,2,128]{3,2,1,0:T(2,128)(2,1)S(1)} %get-tuple-element.27), channel_id=1, source_target_pairs={{1,0},{2,1},{3,2},{4,3},{5,4},{6,5},{7,6},{0,7},{9,8},{10,9},{11,1... | collective-permute-start | bytes 393224 | tf_op jit(solution)/shard_map/ppermute | solution.py:74
  23.8 3.2 %collective-permute-start.2 = (bf16[2,16,16,128]{3,2,1,0:T(8,128)(2,1)S(1)}, bf16[2,16,16,128]{3,2,1,0:T(8,128)(2,1)S(1)}, u32[]{:S(2)}, u32[]{:S(2)}) collective-permute-start(bf16[2,16,16,128]{3,2,1,0:T(8,128)(2,1)S(1)} %get-tuple-element.24), channel_id=1, source_target_pairs={{0,64},{64,128},{128,192},{192,256},{256,320},{320,384},{384,448},... | collective-permute-start | bytes 393224 | tf_op jit(solution)/shard_map/ppermute | solution.py:73
  27.0 3.8 %collective-permute-start.3 = (bf16[2,16,16,128]{3,2,1,0:T(8,128)(2,1)S(1)}, bf16[2,16,16,128]{3,2,1,0:T(8,128)(2,1)S(1)}, u32[]{:S(2)}, u32[]{:S(2)}) collective-permute-start(bf16[2,16,16,128]{3,2,1,0:T(8,128)(2,1)S(1)} %get-tuple-element.25), channel_id=1, source_target_pairs={{64,0},{128,64},{192,128},{256,192},{320,256},{384,320},{448,384},... | collective-permute-start | bytes 393224 | tf_op jit(solution)/shard_map/ppermute | solution.py:74
  30.8 0.5 broadcast.114
  31.4 0.8 reduce.8
  32.3 17.3 %all_to_all.28 = f32[32,1,32]{2,1,0:T(1,128)S(1)} all-to-all(f32[32,1,32]{2,1,0:T(1,128)S(1)} %bitcast.40), channel_id=1, replica_groups=mesh['gx'=8,'gy_0'=4,'gy_1'=2,'gz'=8] {'gx','gy_0'}, dimensions={0} | all-to-all | bytes 8192 | tf_op jit(solution)/shard_map/all_to_all | solution.py:28
  49.6 11.6 %all_to_all.29 = f32[32,1,32]{2,1,0:T(1,128)S(1)} all-to-all(f32[32,1,32]{2,1,0:T(1,128)S(1)} %broadcast_in_dim.10), channel_id=1, replica_groups=mesh['gx'=8,'gy_0'=4,'gy_1'=2,'gz'=8] {'gx','gy_0'}, dimensions={0} | all-to-all | bytes 8192 | tf_op jit(solution)/shard_map/all_to_all | solution.py:40
  61.3 0.8 reshape.44
  62.1 11.6 %all-to-all-start.3 = ((f32[16,1,1024]{2,1,0:T(1,128)}), f32[16,1,1024]{2,1,0:T(1,128)S(1)}, u32[]{:S(2)}, u32[]{:S(2)}) async-start(f32[16,1,1024]{2,1,0:T(1,128)} %reshape.44), calls=%async_computation.3 | async-start | bytes 131072 | tf_op jit(solution)/shard_map/all_to_all | solution.py:40
  73.7 4.2 %fusion.11 = f32[20,20,20,128]{3,2,1,0:T(8,128)} fusion(bf16[16,16,2,128]{3,2,1,0:T(2,128)(2,1)S(1)} %collective-permute-done.5, bf16[16,2,16,128]{3,2,1,0:T(8,128)(2,1)S(1)} %collective-permute-done.4, bf16[16,2,16,128]{3,2,1,0:T(8,128)(2,1)S(1)} %collective-permute-done.1, bf16[16,16,2,128]{3,2,1,0:T(2,128)(2,1)S(1)} %collective-permute-done, ...), kind=kLoop, calls=%fused_computation.20 | loop fusion | flops 30720000 | bytes 5931008 | tf_op jit(solution)/shard_map/convert_element_type | solution.py:120
  77.9 2.9 %all-to-all-done.3 = f32[16,1,1024]{2,1,0:T(1,128)S(1)} async-done(((f32[16,1,1024]{2,1,0:T(1,128)}), f32[16,1,1024]{2,1,0:T(1,128)S(1)}, u32[]{:S(2)}, u32[]{:S(2)}) %all-to-all-start.3) | async-done | bytes 65568 | tf_op jit(solution)/shard_map/all_to_all | solution.py:40
  80.7 0.8 reduce.9
  82.1 11.7 %cholesky.17 = f32[128,128]{1,0:T(8,128)S(1)} custom-call(f32[128,128]{1,0:T(8,128)S(1)} %fusion.40), custom_call_target="Cholesky" | custom-call | tf_op jit(solution)/shard_map/jit(cholesky)/cholesky | solution.py:114
  93.8 0.6 compare_reduce_fusion
  94.5 0.7 fusion.36
  95.2 9.8 %custom-call.6 = f32[1,128,128]{1,2,0:T(8,128)S(1)} custom-call(f32[1,128,128]{2,1,0:T(8,128)S(1)} %fusion.36), custom_call_target="InvertDiagBlocksLowerTriangular" | custom-call | tf_op jit(solution)/shard_map/triangular_solve | solution.py:115
  105.0 0.2 fusion.38
  105.2 2.4 %multiply_reduce_fusion = (f32[128]{0:T(128)S(1)}, f32[4096,128]{0,1:T(8,128)}) fusion(f32[128,128]{1,0:T(8,128)S(1)} %fusion.38, bf16[4096,128]{1,0:T(8,128)(2,1)S(1)} %bitcast.38), kind=kOutput, calls=%fused_computation.50 | convolution fusion | flops 806354816 | bytes 3211776 | tf_op jit(solution)/shard_map/dot_general | solution.py:103
  107.6 1.9 %copy.15 = f32[4096,128]{1,0:T(8,128)S(1)} copy(f32[4096,128]{0,1:T(8,128)} %get-tuple-element.32) | data formatting | bytes 4194304 | tf_op jit(solution)/shard_map/dot_general | solution.py:103
  109.6 18.0 %multiply_reduce_fusion.1 = (f32[128]{0:T(128)S(1)}, f32[128]{0:T(128)S(1)}, f32[16,16,16,128]{3,2,1,0:T(8,128)}) fusion(f32[16,16,16,128]{3,2,1,0:T(8,128)S(1)} %bitcast.36, f32[128,128]{1,0:T(8,128)S(1)} %fusion.38, bf16[16,16,16,128]{3,2,1,0:T(8,128)(2,1)S(1)} %copy-done.1, f32[20,20,20,128]{3,2,1,0:T(8,128)} %fusion.11, f32[16,16,16]{2,1,0:T(8,128)S(1)} %copy-done.3), kind=kOutput, calls=%fused_computation.51 | convolution fusion | flops 822607616 | bytes 30491648 | tf_op jit(solution)/shard_map/dot_general | solution.py:103
  127.5 11.3 %all-reduce.5 = (f32[128]{0:T(128)S(1)}, f32[128]{0:T(128)S(1)}, f32[128]{0:T(128)S(1)}) all-reduce(f32[128]{0:T(128)S(1)} %get-tuple-element.9, f32[128]{0:T(128)S(1)} %get-tuple-element.31, f32[128]{0:T(128)S(1)} %get-tuple-element.8), channel_id=1, replica_groups=mesh['gx'=8,'gy_0'=4,'gy_1'=2,'gz'=8] {'gx'}, use_global_device_ids=true, to_apply=%region_5.6 | all-reduce | flops 384 | bytes 3072 | tf_op jit(solution)/shard_map/psum | solution.py:86
  138.8 6.6 %all-reduce.6 = (f32[128]{0:T(128)S(1)}, f32[128]{0:T(128)S(1)}, f32[128]{0:T(128)S(1)}) all-reduce(f32[128]{0:T(128)S(1)} %get-tuple-element.13, f32[128]{0:T(128)S(1)} %get-tuple-element.14, f32[128]{0:T(128)S(1)} %get-tuple-element.15), channel_id=1, replica_groups=mesh['gx'=8,'gy_0'=4,'gy_1'=2,'gz'=8] {'gy_0'}, use_global_device_ids=true, to_apply=%region_6.7 | all-reduce | flops 384 | bytes 3072 | tf_op jit(solution)/shard_map/psum | solution.py:86
  145.4 8.8 %all-reduce.7 = (f32[128]{0:T(128)S(1)}, f32[128]{0:T(128)S(1)}, f32[128]{0:T(128)S(1)}) all-reduce(f32[128]{0:T(128)S(1)} %get-tuple-element.16, f32[128]{0:T(128)S(1)} %get-tuple-element.17, f32[128]{0:T(128)S(1)} %get-tuple-element.18), channel_id=1, replica_groups=mesh['gx'=8,'gy_0'=4,'gy_1'=2,'gz'=8] {'gy_1'}, use_global_device_ids=true, to_apply=%region_7.8 | all-reduce | flops 384 | bytes 3072 | tf_op jit(solution)/shard_map/psum | solution.py:86
  154.2 11.7 %all-reduce.4 = (f32[128]{0:T(128)S(1)}, f32[128]{0:T(128)S(1)}, f32[128]{0:T(128)S(1)}) all-reduce(f32[128]{0:T(128)S(1)} %get-tuple-element.19, f32[128]{0:T(128)S(1)} %get-tuple-element.20, f32[128]{0:T(128)S(1)} %get-tuple-element.21), channel_id=1, replica_groups=mesh['gx'=8,'gy_0'=4,'gy_1'=2,'gz'=8] {'gz'}, use_global_device_ids=true, to_apply=%region_8.9 | all-reduce | flops 384 | bytes 3072 | tf_op jit(solution)/shard_map/psum | solution.py:86
  165.9 0.5 add_sqrt_fusion
  166.4 2.8 %subtract_convert_fusion = bf16[16,16,16,128]{3,2,1,0:T(8,128)(2,1)} fusion(f32[16,16,16,128]{3,2,1,0:T(8,128)} %get-tuple-element.30, f32[128]{0:T(128)S(1)} %get-tuple-element.23, f32[4096,128]{1,0:T(8,128)S(1)} %copy.15), kind=kLoop, calls=%fused_computation.52 | loop fusion | flops 1572864 | bytes 5243392 | tf_op jit(solution)/shard_map/convert_element_type | solution.py:135
  (32 shorter events, 1.0 us)
Async XLA Ops:
  0.6 15.0 %copy-start.1 = (bf16[16,16,16,128]{3,2,1,0:T(8,128)(2,1)S(1)}, bf16[16,16,16,128]{3,2,1,0:T(8,128)(2,1)}, u32[]{:S(2)}) copy-start(bf16[16,16,16,128]{3,2,1,0:T(8,128)(2,1)} %param.2) | copy-start | bytes 3145732
  3.8 27.1 %all-to-all-start = ((f32[16,1,1024]{2,1,0:T(1,128)}), f32[16,1,1024]{2,1,0:T(1,128)S(1)}, u32[]{:S(2)}, u32[]{:S(2)}) async-start(f32[16,1,1024]{2,1,0:T(1,128)} %reshape.42), calls=%async_computation | async-start | bytes 131072 | tf_op jit(solution)/shard_map/all_to_all | solution.py:21
  15.6 11.4 %collective-permute-start.1 = (bf16[16,2,16,128]{3,2,1,0:T(8,128)(2,1)S(1)}, bf16[16,2,16,128]{3,2,1,0:T(8,128)(2,1)S(1)}, u32[]{:S(2)}, u32[]{:S(2)}) collective-permute-start(bf16[16,2,16,128]{3,2,1,0:T(8,128)(2,1)S(1)} %get-tuple-element.28), channel_id=1, source_target_pairs={{0,8},{8,16},{16,24},{24,32},{32,40},{40,48},{48,56},{56,0},{1,9},... | collective-permute-start | bytes 393224 | tf_op jit(solution)/shard_map/ppermute | solution.py:73
  16.8 56.8 %collective-permute-start.4 = (bf16[16,2,16,128]{3,2,1,0:T(8,128)(2,1)S(1)}, bf16[16,2,16,128]{3,2,1,0:T(8,128)(2,1)S(1)}, u32[]{:S(2)}, u32[]{:S(2)}) collective-permute-start(bf16[16,2,16,128]{3,2,1,0:T(8,128)(2,1)S(1)} %get-tuple-element.29), channel_id=1, source_target_pairs={{8,0},{16,8},{24,16},{32,24},{40,32},{48,40},{56,48},{0,56},{9,1},... | collective-permute-start | bytes 393224 | tf_op jit(solution)/shard_map/ppermute | solution.py:74
  17.1 56.6 %collective-permute-start = (bf16[16,16,2,128]{3,2,1,0:T(2,128)(2,1)S(1)}, bf16[16,16,2,128]{3,2,1,0:T(2,128)(2,1)S(1)}, u32[]{:S(2)}, u32[]{:S(2)}) collective-permute-start(bf16[16,16,2,128]{3,2,1,0:T(2,128)(2,1)S(1)} %get-tuple-element.26), channel_id=1, source_target_pairs={{0,1},{1,2},{2,3},{3,4},{4,5},{5,6},{6,7},{7,0},{8,9},{9,10},{10,1... | collective-permute-start | bytes 393224 | tf_op jit(solution)/shard_map/ppermute | solution.py:73
  20.6 53.0 %collective-permute-start.5 = (bf16[16,16,2,128]{3,2,1,0:T(2,128)(2,1)S(1)}, bf16[16,16,2,128]{3,2,1,0:T(2,128)(2,1)S(1)}, u32[]{:S(2)}, u32[]{:S(2)}) collective-permute-start(bf16[16,16,2,128]{3,2,1,0:T(2,128)(2,1)S(1)} %get-tuple-element.27), channel_id=1, source_target_pairs={{1,0},{2,1},{3,2},{4,3},{5,4},{6,5},{7,6},{0,7},{9,8},{10,9},{11,1... | collective-permute-start | bytes 393224 | tf_op jit(solution)/shard_map/ppermute | solution.py:74
  23.8 49.9 %collective-permute-start.2 = (bf16[2,16,16,128]{3,2,1,0:T(8,128)(2,1)S(1)}, bf16[2,16,16,128]{3,2,1,0:T(8,128)(2,1)S(1)}, u32[]{:S(2)}, u32[]{:S(2)}) collective-permute-start(bf16[2,16,16,128]{3,2,1,0:T(8,128)(2,1)S(1)} %get-tuple-element.24), channel_id=1, source_target_pairs={{0,64},{64,128},{128,192},{192,256},{256,320},{320,384},{384,448},... | collective-permute-start | bytes 393224 | tf_op jit(solution)/shard_map/ppermute | solution.py:73
  27.0 46.7 %collective-permute-start.3 = (bf16[2,16,16,128]{3,2,1,0:T(8,128)(2,1)S(1)}, bf16[2,16,16,128]{3,2,1,0:T(8,128)(2,1)S(1)}, u32[]{:S(2)}, u32[]{:S(2)}) collective-permute-start(bf16[2,16,16,128]{3,2,1,0:T(8,128)(2,1)S(1)} %get-tuple-element.25), channel_id=1, source_target_pairs={{64,0},{128,64},{192,128},{256,192},{320,256},{384,320},{448,384},... | collective-permute-start | bytes 393224 | tf_op jit(solution)/shard_map/ppermute | solution.py:74
  62.1 18.7 %all-to-all-start.3 = ((f32[16,1,1024]{2,1,0:T(1,128)}), f32[16,1,1024]{2,1,0:T(1,128)S(1)}, u32[]{:S(2)}, u32[]{:S(2)}) async-start(f32[16,1,1024]{2,1,0:T(1,128)} %reshape.44), calls=%async_computation.3 | async-start | bytes 131072 | tf_op jit(solution)/shard_map/all_to_all | solution.py:40
  107.6 2.0 %copy-start.3 = (f32[16,16,16]{2,1,0:T(8,128)S(1)}, f32[16,16,16]{2,1,0:T(8,128)}, u32[]{:S(2)}) copy-start(f32[16,16,16]{2,1,0:T(8,128)} %param.3) | copy-start | bytes 49156
  109.5 56.9 %copy-start = (f32[4096,128]{1,0:T(8,128)}, f32[4096,128]{1,0:T(8,128)S(1)}, u32[]{:S(2)}) copy-start(f32[4096,128]{1,0:T(8,128)S(1)} %copy.15) | copy-start | bytes 6291460
  166.4 2.8 %copy-start.2 = (f32[128]{0:T(128)}, f32[128]{0:T(128)S(1)}, u32[]{:S(2)}) copy-start(f32[128]{0:T(128)S(1)} %get-tuple-element.23) | copy-start | bytes 1540
where the time goes:
time: 172 us; the launch traced here: 169 us
  blocking collectives  67.2 us (39%)
  starting transfers between devices  38.3 us (22%)
  other arithmetic  32.1 us (19%)
  matrix products  22.7 us (13%)
  local copies, waits for them, and re-layouts  5.12 us (3%)
  waiting for transfers between devices  2.88 us (2%)
    psum x4, blocking collectives, by_axis(): return functools.reduce(lax.psum, axes, value)  38.3 us
    dot_general x2, matrix products, rotate(): jnp.dot(flat, inverse.T, precision=lax.Precision.HIGHEST).reshape(shape)  20.3 us
    all_to_all x1, blocking collectives, sum_in_two_steps(): return jnp.sum(lax.all_to_all(own, far, 0, 0, tiled=True), axis=0)  17.3 us
    another operation x3, other arithmetic, local(): factor = jnp.linalg.cholesky(correlation)  12.4 us
    all_to_all x1, starting transfers between devices, sum_at_owner(): blocks = lax.all_to_all(split_up(value, dim, count), axis, 0, 0, tiled=True)  11.8 us
    all_to_all x1, blocking collectives, copy_for_each(): return lax.all_to_all(copies, axis, split_axis=0, concat_axis=0, tiled=True)  11.6 us
    all_to_all x1, starting transfers between devices, copy_for_each(): return lax.all_to_all(copies, axis, split_axis=0, concat_axis=0, tiled=True)  11.6 us
    another operation x2, other arithmetic, local(): lax.linalg.triangular_solve(factor, jnp.eye(bands, dtype=jnp.float32), le...  10.5 us
  transfers between devices with their start and end apart: 8, of which 1 were waited for; matrix products, arithmetic and copies ran while one was open for 4% of the time, Pallas kernels for 0%

commit v1 on v0

v1 whole, which is shorter than its diff:
```python
import functools

import jax
import jax.numpy as jnp
import numpy as np
from jax import lax
from jax.experimental import pallas as pl
from jax.experimental.pallas import tpu as pltpu
from jax.sharding import Mesh
from jax.sharding import PartitionSpec as P

GX = ("gx",)
GY = ("gy_0", "gy_1")
GZ = ("gz",)
NEAR = ("gy_0", "gz")
FAR = ("gx", "gy_1")
HIGHEST = lax.Precision.HIGHEST
CHUNKS = 4


def plane_weights(cy, cz):
    side = {0: 90.0, 1: -16.0, 2: 1.0}
    weights = np.zeros((cy * cz, cy * cz + 4 * cz + 4 * cy), np.float32)
    for y in range(cy):
        for z in range(cz):
            row = y * cz + z
            weights[row, row] = side[0]
            for step in (-2, -1, 1, 2):
                w = side[abs(step)]
                base = cy * cz
                if 0 <= y + step < cy:
                    weights[row, row + step * cz] = w
                elif y + step < 0:
                    weights[row, base + (y + step + 2) * cz + z] = w
                else:
                    weights[row, base + 2 * cz + (y + step - cy) * cz + z] = w
                base = cy * cz + 4 * cz
                if 0 <= z + step < cz:
                    weights[row, row + step] = w
                elif z + step < 0:
                    weights[row, base + y * 2 + z + step + 2] = w
                else:
                    weights[row, base + 2 * cy + y * 2 + z + step - cz] = w
    return weights


def over_cells(left, right):
    return lax.dot_general(
        left, right, (((0,), (0,)), ((), ())), preferred_element_type=jnp.float32
    )


def iotas(rows, columns):
    shape = (rows, columns)
    return lax.broadcasted_iota(jnp.int32, shape, 0), lax.broadcasted_iota(jnp.int32, shape, 1)


def apply_kernel(p, xlo, xhi, ylo, yhi, zlo, zhi, pot, weights, high, low, sums):
    cx, cells, bands = p.shape
    stencil = weights[...]
    total = None
    for x in range(cx):
        def plane(at):
            ref, at = (xlo, at + 2) if at < 0 else (xhi, at - cx) if at >= cx else (p, at)
            return ref[at].astype(jnp.float32)

        own = p[x]
        around = jnp.concatenate([own, ylo[x], yhi[x], zlo[x], zhi[x]], axis=0)
        kinetic = jnp.dot(stencil, around, preferred_element_type=jnp.float32)
        kinetic = kinetic + (plane(x - 2) + plane(x + 2)) - 16.0 * (plane(x - 1) + plane(x + 1))
        given = own.astype(jnp.float32)
        applied = kinetic * (1.0 / 24.0) + pot[:, x : x + 1] * given
        top = applied.astype(jnp.bfloat16)
        rest = (applied - top.astype(jnp.float32)).astype(jnp.bfloat16)
        high[x] = top
        low[x] = rest
        part = over_cells(
            jnp.concatenate([own, top], axis=1), jnp.concatenate([own, top, rest], axis=1)
        )
        total = part if total is None else total + part
    b = bands
    row, column = iotas(b, b)
    gram = total[:b, :b]
    cross = total[:b, b : 2 * b] + total[:b, 2 * b :]
    rest = total[b:, 2 * b :]
    square = total[b:, b : 2 * b] + rest + rest.T
    cross_own = jnp.sum(jnp.where(row == column, cross, 0.0), axis=0, keepdims=True)
    cross = cross + cross.T
    sums[:b] = jnp.where(row >= column, gram, cross)
    spare = jnp.where(row == 0, cross_own, pltpu.roll(jnp.broadcast_to(cross_own, (b, b)), b - 1, 1))
    sums[b:] = jnp.where(row > column, 2.0 * square, jnp.where(row == column, square, spare))


def across(value, lane):
    return jnp.broadcast_to(value[:, lane : lane + 1], value.shape)


def down(value, row):
    return jnp.broadcast_to(value[row : row + 1, :], value.shape)


def inverse_factor(rows):
    count = len(rows)
    size, bands = rows[0].shape
    row, column = iotas(size, bands)
    rows = list(rows)
    right = [jnp.where(column == row + size * k, 1.0, 0.0) for k in range(count)]
    done = []
    for k in range(count):
        own = [across(rows[k], size * k + c) for c in range(size)]
        below = {
            i: [across(rows[i], size * k + c) for c in range(size)] for i in range(k + 1, count)
        }
        left_k, right_k = rows[k], right[k]
        result = jnp.zeros_like(right_k)
        pivots = []
        for c in range(size):
            pivot = down(own[c], c)
            share = 1.0 / pivot
            left_row, right_row = down(left_k, c), down(right_k, c)
            pivots.append((left_row, right_row))
            result = jnp.where(row == c, right_row * lax.rsqrt(pivot), result)
            factor = jnp.where(row > c, own[c] * share, 0.0)
            left_k = left_k - factor * left_row
            right_k = right_k - factor * right_row
            entries = [down(own[d], c) for d in range(c + 1, size)]
            for d, entry in zip(range(c + 1, size), entries):
                own[d] = own[d] - factor * entry
            for lines in below.values():
                lines[c] = lines[c] * share
                for d, entry in zip(range(c + 1, size), entries):
                    lines[d] = lines[d] - lines[c] * entry
        done.append(result)
        for i, lines in below.items():
            for line, (left_row, right_row) in zip(lines, pivots):
                rows[i] = rows[i] - line * left_row
                right[i] = right[i] - line * right_row
    return done


def split_3(value):
    parts = []
    for _ in range(3):
        part = value.astype(jnp.bfloat16)
        value = value - part.astype(jnp.float32)
        parts.append(part)
    return parts


def finish_kernel(
    cells, sums, p, high, low, rotated, residual, quotients, norms, w, w_low, out_r, out_s, sems
):
    rows, bands = p.shape
    row, column = iotas(bands, bands)
    scale = 1.0 / cells
    first, second = sums[:bands] * scale, sums[bands:] * scale
    lower = jnp.where(row >= column, first, 0.0)
    gram = lower + jnp.where(row > column, first, 0.0).T
    own = jnp.where(column[:1] == 0, pltpu.roll(second[:8], 1, 1)[1:2], second[:1])
    cross = jnp.where(row < column, first, jnp.where(row == column, own, 0.0))
    square = jnp.where(row >= column, second, 0.0)
    size = 8
    inverse = jnp.concatenate(
        inverse_factor([gram[i : i + size] for i in range(0, bands, size)]), axis=0
    )

    def diagonal(matrix):
        product = jnp.dot(inverse, matrix, precision=HIGHEST, preferred_element_type=jnp.float32)
        return jnp.sum(product * inverse, axis=1, keepdims=True)

    quotient = diagonal(cross)
    squares = diagonal(square) - quotient * quotient * (2.0 - diagonal(gram))
    norm = jnp.sqrt(jnp.maximum(squares, 0.0) + 1e-06)
    quotients[...] = jnp.broadcast_to(quotient, (bands, bands)).T[:8]
    norms[...] = jnp.broadcast_to(norm, (bands, bands)).T[:8]

    turned = inverse.T
    shifted = (-quotient * inverse).T
    none = jnp.zeros((bands, bands), jnp.bfloat16)
    for at, (a, s) in enumerate(zip(split_3(turned), split_3(shifted))):
        w[at, :bands, :bands] = a
        w[at, :bands, bands:] = s
        w[at, bands:, :bands] = none
        w[at, bands:, bands:] = a
        if at < 2:
            w_low[at * bands : (at + 1) * bands] = a
    step = rows // CHUNKS
    copies = []
    for chunk in range(CHUNKS):
        part = pl.ds(chunk * step, step)
        both = jnp.concatenate([p[part], high[part]], axis=1)
        rest = low[part]
        result = jnp.dot(both, w[2], preferred_element_type=jnp.float32)
        result = result + jnp.dot(both, w[1], preferred_element_type=jnp.float32)
        result = result + jnp.dot(both, w[0], preferred_element_type=jnp.float32)
        extra = jnp.dot(
            jnp.concatenate([rest, rest], axis=1), w_low[...], preferred_element_type=jnp.float32
        )
        out_r[part] = result[:, :bands]
        out_s[part] = (result[:, bands:] + extra).astype(jnp.bfloat16)
        for at, (source, target) in enumerate(((out_r, rotated), (out_s, residual))):
            copy = pltpu.make_async_copy(source.at[part], target.at[part], sems.at[chunk, at])
            copy.start()
            copies.append(copy)
    for copy in copies:
        copy.wait()


def vmem(count):
    return [pl.BlockSpec(memory_space=pltpu.VMEM)] * count


def from_neighbours(low_edge, high_edge, axes):
    count = lax.axis_size(axes)
    up = [(i, (i + 1) % count) for i in range(count)]
    return (
        lax.ppermute(high_edge, axes, up),
        lax.ppermute(low_edge, axes, [(b, a) for a, b in up]),
    )


def exchange(blocks, axes):
    return lax.all_to_all(blocks, axes, split_axis=0, concat_axis=0, tiled=True)


def for_each(value, axes):
    return exchange(jnp.broadcast_to(value, (lax.axis_size(axes), *value.shape)), axes)


def sum_everywhere(value):
    rows, columns = value.shape
    own = jnp.sum(exchange(value.reshape(lax.axis_size(NEAR), -1, columns), NEAR), axis=0)
    own = jnp.sum(for_each(own, FAR), axis=0)
    return for_each(own, NEAR).reshape(rows, columns)


def local(wavefunctions, potential):
    cx, cy, cz, bands = wavefunctions.shape
    cells = cx * cy * cz
    total_cells = cells * lax.axis_size(GX) * lax.axis_size(GY) * lax.axis_size(GZ)
    planes = wavefunctions.reshape(cx, cy * cz, bands)
    ylo, yhi = from_neighbours(
        wavefunctions[:, :2].reshape(cx, 2 * cz, bands),
        wavefunctions[:, cy - 2 :].reshape(cx, 2 * cz, bands),
        GY,
    )
    xlo, xhi = from_neighbours(planes[:2], planes[cx - 2 :], GX)
    zlo, zhi = from_neighbours(
        wavefunctions[:, :, :2].reshape(cx, 2 * cy, bands),
        wavefunctions[:, :, cz - 2 :].reshape(cx, 2 * cy, bands),
        GZ,
    )
    weights = jnp.asarray(plane_weights(cy, cz), jnp.bfloat16)
    shape = (cx, cy * cz, bands)
    high, low, sums = pl.pallas_call(
        apply_kernel,
        out_shape=(
            jax.ShapeDtypeStruct(shape, jnp.bfloat16),
            jax.ShapeDtypeStruct(shape, jnp.bfloat16),
            jax.ShapeDtypeStruct((2 * bands, bands), jnp.float32),
        ),
        in_specs=vmem(9),
        out_specs=tuple(vmem(3)),
        name="apply",
    )(planes, xlo, xhi, ylo, yhi, zlo, zhi, potential.reshape(cx, cy * cz).T, weights)
    sums = sum_everywhere(sums)
    flat = (cells, bands)
    kept = pl.BlockSpec(memory_space=pl.ANY)
    rotated, residual, quotients, norms = pl.pallas_call(
        functools.partial(finish_kernel, total_cells),
        out_shape=(
            jax.ShapeDtypeStruct(flat, jnp.float32),
            jax.ShapeDtypeStruct(flat, jnp.bfloat16),
            jax.ShapeDtypeStruct((8, bands), jnp.float32),
            jax.ShapeDtypeStruct((8, bands), jnp.float32),
        ),
        in_specs=vmem(4),
        out_specs=(kept, kept, *vmem(2)),
        scratch_shapes=[
            pltpu.VMEM((3, 2 * bands, 2 * bands), jnp.bfloat16),
            pltpu.VMEM((2 * bands, bands), jnp.bfloat16),
            pltpu.VMEM(flat, jnp.float32),
            pltpu.VMEM(flat, jnp.bfloat16),
            pltpu.SemaphoreType.DMA((CHUNKS, 2)),
        ],
        name="finish",
    )(sums, planes.reshape(flat), high.reshape(flat), low.reshape(flat))
    whole = (cx, cy, cz, bands)
    return rotated.reshape(whole), residual.reshape(whole), quotients[0], norms[0]


def solution(mesh):
    torus = Mesh(
        mesh.devices.reshape(mesh.shape["gx"], 4, 2, mesh.shape["gz"]), ("gx", "gy_0", "gy_1", "gz")
    )
    return jax.shard_map(
        local,
        mesh=torus,
        in_specs=(P("gx", GY, "gz", None), P("gx", GY, "gz")),
        out_specs=(P("gx", GY, "gz", None), P("gx", GY, "gz", None), P(), P()),
        check_vma=False,
    )
```

time: 172 us -> 96.1 us (0.56); the launches traced: 169 us -> 95.6 us
  other arithmetic: 32.1 us -> 0.05 us
  matrix products: 22.7 us -> 0 us
  blocking collectives: 67.2 us -> 47.4 us
  Pallas kernels: 0 us -> 17.7 us
  starting transfers between devices: 38.3 us -> 22.5 us
  waiting for transfers between devices: 2.88 us -> 0.21 us
  local copies, waits for them, and re-layouts: 5.12 us -> 6.95 us
    psum x4 -> x0, blocking collectives: 38.3 us -> none  [by_axis(): return functools.reduce(lax.psum, axes, value)]
    all_to_all x2 -> x0, starting transfers between devices: 23.4 us -> none  [the longest x1 11.8 us: sum_at_owner(): blocks = lax.all_to_all(split_up(value, dim, count), axis, 0, 0, tiled=True)]
    another operation x5 -> x0, other arithmetic: 22.9 us -> none  [the longest x3 12.4 us: local(): factor = jnp.linalg.cholesky(correlation)]
    dot_general x3 -> x0, matrix products: 22.4 us -> none  [the longest x2 20.3 us: rotate(): jnp.dot(flat, inverse.T, precision=lax.Precision.HIGHEST).reshape(shape)]
    all_to_all x2 -> x3, blocking collectives: 28.9 us -> 47.4 us  [exchange(): return lax.all_to_all(blocks, axes, split_axis=0, concat_axis=0, tiled=True)]
    pallas_call x0 -> x2, Pallas kernels: none -> 17.7 us  [the longest x1 10.4 us: local(): pl.pallas_call(functools.partial(finish_kernel, total_cells), out_shape=(...]
    ppermute x6, starting transfers between devices: 14.9 us -> 22.5 us  [the longest x3 14.5 us: from_neighbours(): lax.ppermute(low_edge, axes, [(b, a) for a, b in up])]
    convert_element_type x2 -> x0, other arithmetic: 7.06 us -> none  [the longest x1 4.21 us: local(): raw_applied = stencil(raw_padded.astype(jnp.float32), given, potential)]
  transfers between devices with their start and end apart: 8 -> 6, of which waited for: 1 -> 1; matrix products, arithmetic and copies ran while one was open for 4% -> 4% of each run, Pallas kernels for 0% -> 0%
where the time goes in v1:
time: 96.1 us; the launch traced here: 95.6 us
  blocking collectives  47.4 us (49%)
  starting transfers between devices  22.5 us (23%)
  Pallas kernels  17.7 us (18%)
  local copies, waits for them, and re-layouts  6.95 us (7%)
    all_to_all x3, blocking collectives, exchange(): return lax.all_to_all(blocks, axes, split_axis=0, concat_axis=0, tiled=True)  47.4 us
    ppermute x3, starting transfers between devices, from_neighbours(): lax.ppermute(low_edge, axes, [(b, a) for a, b in up])  14.5 us
    pallas_call x1, Pallas kernels, local(): pl.pallas_call(functools.partial(finish_kernel, total_cells), out_shape=(...  10.4 us
    ppermute x3, starting transfers between devices, from_neighbours(): lax.ppermute(high_edge, axes, up)  8.01 us
    pallas_call x1, Pallas kernels, local(): pl.pallas_call(apply_kernel, out_shape=(jax.ShapeDtypeStruct(shape, jnp.b...  7.26 us
    unnamed x13, local copies, waits for them, and re-layouts  2.33 us
  transfers between devices with their start and end apart: 6, of which 1 were waited for; matrix products, arithmetic and copies ran while one was open for 4% of the time, Pallas kernels for 0%

profile of v1, /device:TPU:1, one launch (start us, length us, event | category | flops | bytes accessed | tf_op | source)
XLA Modules:
  0.0 95.6 jit_solution(11660244511613033765)
XLA Ops:
  0.6 1.0 %fusion.2 = (bf16[2,16,16,128]{3,2,1,0:T(8,128)(2,1)S(1)}, bf16[2,16,16,128]{3,2,1,0:T(8,128)(2,1)S(1)}) fusion(bf16[16,16,16,128]{3,2,1,0:T(8,128)(2,1)} %param.3), kind=kLoop, calls=%fused_computation.4 | loop fusion | bytes 524288 | tf_op jit(solution)/shard_map/slice | solution.py:247
  1.6 4.0 %collective-permute-start = (bf16[2,256,128]{2,1,0:T(8,128)(2,1)S(1)}, bf16[2,256,128]{2,1,0:T(8,128)(2,1)S(1)}, u32[]{:S(2)}, u32[]{:S(2)}) collective-permute-start(bf16[2,256,128]{2,1,0:T(8,128)(2,1)S(1)} %bitcast.32), channel_id=1, source_target_pairs={{0,64},{64,128},{128,192},{192,256},{256,320},{320,384},{384,448},... | collective-permute-start | bytes 393224 | tf_op jit(solution)/shard_map/ppermute | solution.py:217
  5.7 3.8 %collective-permute-start.1 = (bf16[2,256,128]{2,1,0:T(8,128)(2,1)S(1)}, bf16[2,256,128]{2,1,0:T(8,128)(2,1)S(1)}, u32[]{:S(2)}, u32[]{:S(2)}) collective-permute-start(bf16[2,256,128]{2,1,0:T(8,128)(2,1)S(1)} %bitcast.28), channel_id=1, source_target_pairs={{64,0},{128,64},{192,128},{256,192},{320,256},{384,320},{448,384},... | collective-permute-start | bytes 393224 | tf_op jit(solution)/shard_map/ppermute | solution.py:218
  9.5 1.0 %fusion.1 = (bf16[16,2,16,128]{3,2,1,0:T(8,128)(2,1)S(1)}, bf16[16,2,16,128]{3,2,1,0:T(8,128)(2,1)S(1)}) fusion(bf16[16,16,16,128]{3,2,1,0:T(8,128)(2,1)} %param.3), kind=kLoop, calls=%fused_computation.3 | loop fusion | bytes 524288 | tf_op jit(solution)/shard_map/slice | solution.py:243
  10.5 2.1 %collective-permute-start.2 = (bf16[16,32,128]{2,1,0:T(8,128)(2,1)S(1)}, bf16[16,32,128]{2,1,0:T(8,128)(2,1)S(1)}, u32[]{:S(2)}, u32[]{:S(2)}) collective-permute-start(bf16[16,32,128]{2,1,0:T(8,128)(2,1)S(1)} %bitcast.30), channel_id=1, source_target_pairs={{0,8},{8,16},{16,24},{24,32},{32,40},{40,48},{48,56},{56,0},{1,9},... | collective-permute-start | bytes 393224 | tf_op jit(solution)/shard_map/ppermute | solution.py:217
  12.5 4.0 %collective-permute-start.3 = (bf16[16,32,128]{2,1,0:T(8,128)(2,1)S(1)}, bf16[16,32,128]{2,1,0:T(8,128)(2,1)S(1)}, u32[]{:S(2)}, u32[]{:S(2)}) collective-permute-start(bf16[16,32,128]{2,1,0:T(8,128)(2,1)S(1)} %bitcast.29), channel_id=1, source_target_pairs={{8,0},{16,8},{24,16},{32,24},{40,32},{48,40},{56,48},{0,56},{9,1},... | collective-permute-start | bytes 393224 | tf_op jit(solution)/shard_map/ppermute | solution.py:218
  16.6 1.4 %fusion = (bf16[16,16,2,128]{3,2,1,0:T(2,128)(2,1)S(1)}, bf16[16,16,2,128]{3,2,1,0:T(2,128)(2,1)S(1)}) fusion(bf16[16,16,16,128]{3,2,1,0:T(8,128)(2,1)} %param.3), kind=kLoop, calls=%fused_computation.2 | loop fusion | bytes 524288 | tf_op jit(solution)/shard_map/slice | solution.py:249
  18.0 1.9 %collective-permute-start.4 = (bf16[16,32,128]{2,1,0:T(8,128)(2,1)S(1)}, bf16[16,32,128]{2,1,0:T(8,128)(2,1)S(1)}, u32[]{:S(2)}, u32[]{:S(2)}) collective-permute-start(bf16[16,32,128]{2,1,0:T(8,128)(2,1)S(1)} %bitcast.33), channel_id=1, source_target_pairs={{0,1},{1,2},{2,3},{3,4},{4,5},{5,6},{6,7},{7,0},{8,9},{9,10},{10,1... | collective-permute-start | bytes 393224 | tf_op jit(solution)/shard_map/ppermute | solution.py:217
  19.9 0.0 collective-permute-done.xlo
  19.9 0.0 copy-start
  19.9 6.6 %collective-permute-start.5 = (bf16[16,32,128]{2,1,0:T(8,128)(2,1)S(1)}, bf16[16,32,128]{2,1,0:T(8,128)(2,1)S(1)}, u32[]{:S(2)}, u32[]{:S(2)}) collective-permute-start(bf16[16,32,128]{2,1,0:T(8,128)(2,1)S(1)} %bitcast.31), channel_id=1, source_target_pairs={{1,0},{2,1},{3,2},{4,3},{5,4},{6,5},{7,6},{0,7},{9,8},{10,9},{11,1... | collective-permute-start | bytes 393224 | tf_op jit(solution)/shard_map/ppermute | solution.py:218
  26.6 1.7 %copy.8 = f32[16,16,16]{0,2,1:T(8,128)} copy(f32[16,16,16]{2,1,0:T(8,128)} %param.4) | data formatting | bytes 32768 | tf_op args[1]
  28.2 0.0 collective-permute-done.1.xhi
  28.2 0.0 collective-permute-done.2.ylo
  28.3 0.0 copy-start.2
  28.3 0.0 collective-permute-done.3.yhi
  28.3 0.0 copy-start.3
  28.3 0.0 collective-permute-done.4.zlo
  28.3 0.0 copy-start.4
  28.3 0.2 collective-permute-done.5.zhi
  28.5 0.0 copy-done
  28.5 0.4 copy-done.1
  28.9 0.0 copy-done.2
  28.9 0.0 copy-done.3
  29.0 0.0 copy-done.4
  29.0 0.1 copy-done.5
  29.2 7.3 %apply.1 = (bf16[16,256,128]{2,1,0:T(8,128)(2,1)}, bf16[16,256,128]{2,1,0:T(8,128)(2,1)}, f32[256,128]{1,0:T(8,128)}) custom-call(bf16[16,256,128]{2,1,0:T(8,128)(2,1)} %bitcast.21, bf16[2,256,128]{2,1,0:T(8,128)(2,1)} %copy-done, bf16[2,256,128]{2,1,0:T(8,128)(2,1)} %copy-done.1, bf16[16,32,128]{2,1,0:T(8,128)(2,1)} %copy-done.2, ...), custom_call_target="tpu_custom_call" | custom-call | tf_op jit(solution)/shard_map/apply/pallas_call | solution.py:255
  36.4 16.4 %all_to_all.15 = f32[32,8,128]{2,1,0:T(8,128)S(1)} all-to-all(f32[32,8,128]{2,1,0:T(8,128)} %bitcast.27), channel_id=1, replica_groups=mesh['gx'=8,'gy_0'=4,'gy_1'=2,'gz'=8] {'gy_0','gz'}, dimensions={0} | all-to-all | bytes 262144 | tf_op jit(solution)/shard_map/all_to_all | solution.py:223
  52.9 18.2 %all_to_all.16 = f32[16,8,128]{2,1,0:T(8,128)S(1)} all-to-all(f32[16,8,128]{2,1,0:T(8,128)S(1)} %broadcast_in_dim.6), channel_id=1, replica_groups=mesh['gx'=8,'gy_0'=4,'gy_1'=2,'gz'=8] {'gx','gy_1'}, dimensions={0} | all-to-all | bytes 131072 | tf_op jit(solution)/shard_map/all_to_all | solution.py:223
  71.1 12.8 %all_to_all.17 = f32[32,8,128]{2,1,0:T(8,128)} all-to-all(f32[32,8,128]{2,1,0:T(8,128)S(1)} %broadcast_in_dim.7), channel_id=1, replica_groups=mesh['gx'=8,'gy_0'=4,'gy_1'=2,'gz'=8] {'gy_0','gz'}, dimensions={0} | all-to-all | bytes 262144 | tf_op jit(solution)/shard_map/all_to_all | solution.py:223
  83.9 10.4 %finish.1 = (f32[4096,128]{1,0:T(8,128)}, bf16[4096,128]{1,0:T(8,128)(2,1)}, f32[8,128]{1,0:T(8,128)}, f32[8,128]{1,0:T(8,128)}) custom-call(f32[256,128]{1,0:T(8,128)} %bitcast.26, bf16[4096,128]{1,0:T(8,128)(2,1)} %bitcast.22, bf16[4096,128]{1,0:T(8,128)(2,1)} %bitcast.23, bf16[4096,128]{1,0:T(8,128)(2,1)} %bitcast.24), custom_call_target="tpu_custom_call" | custom-call | tf_op jit(solution)/shard_map/finish/pallas_call | solution.py:269
  94.4 1.2 %slice_bitcast_fusion = (f32[128]{0:T(128)}, f32[128]{0:T(128)}) fusion(f32[8,128]{1,0:T(8,128)} %get-tuple-element.17, f32[8,128]{1,0:T(8,128)} %get-tuple-element.16), kind=kLoop, calls=%fused_computation | loop fusion | bytes 2048 | tf_op jit(solution)/shard_map/squeeze | solution.py:289
  (6 shorter events, 0.1 us)
Async XLA Ops:
  1.6 18.3 %collective-permute-start = (bf16[2,256,128]{2,1,0:T(8,128)(2,1)S(1)}, bf16[2,256,128]{2,1,0:T(8,128)(2,1)S(1)}, u32[]{:S(2)}, u32[]{:S(2)}) collective-permute-start(bf16[2,256,128]{2,1,0:T(8,128)(2,1)S(1)} %bitcast.32), channel_id=1, source_target_pairs={{0,64},{64,128},{128,192},{192,256},{256,320},{320,384},{384,448},... | collective-permute-start | bytes 393224 | tf_op jit(solution)/shard_map/ppermute | solution.py:217
  5.7 22.6 %collective-permute-start.1 = (bf16[2,256,128]{2,1,0:T(8,128)(2,1)S(1)}, bf16[2,256,128]{2,1,0:T(8,128)(2,1)S(1)}, u32[]{:S(2)}, u32[]{:S(2)}) collective-permute-start(bf16[2,256,128]{2,1,0:T(8,128)(2,1)S(1)} %bitcast.28), channel_id=1, source_target_pairs={{64,0},{128,64},{192,128},{256,192},{320,256},{384,320},{448,384},... | collective-permute-start | bytes 393224 | tf_op jit(solution)/shard_map/ppermute | solution.py:218
  10.5 17.8 %collective-permute-start.2 = (bf16[16,32,128]{2,1,0:T(8,128)(2,1)S(1)}, bf16[16,32,128]{2,1,0:T(8,128)(2,1)S(1)}, u32[]{:S(2)}, u32[]{:S(2)}) collective-permute-start(bf16[16,32,128]{2,1,0:T(8,128)(2,1)S(1)} %bitcast.30), channel_id=1, source_target_pairs={{0,8},{8,16},{16,24},{24,32},{32,40},{40,48},{48,56},{56,0},{1,9},... | collective-permute-start | bytes 393224 | tf_op jit(solution)/shard_map/ppermute | solution.py:217
  12.5 15.7 %collective-permute-start.3 = (bf16[16,32,128]{2,1,0:T(8,128)(2,1)S(1)}, bf16[16,32,128]{2,1,0:T(8,128)(2,1)S(1)}, u32[]{:S(2)}, u32[]{:S(2)}) collective-permute-start(bf16[16,32,128]{2,1,0:T(8,128)(2,1)S(1)} %bitcast.29), channel_id=1, source_target_pairs={{8,0},{16,8},{24,16},{32,24},{40,32},{48,40},{56,48},{0,56},{9,1},... | collective-permute-start | bytes 393224 | tf_op jit(solution)/shard_map/ppermute | solution.py:218
  18.0 10.3 %collective-permute-start.4 = (bf16[16,32,128]{2,1,0:T(8,128)(2,1)S(1)}, bf16[16,32,128]{2,1,0:T(8,128)(2,1)S(1)}, u32[]{:S(2)}, u32[]{:S(2)}) collective-permute-start(bf16[16,32,128]{2,1,0:T(8,128)(2,1)S(1)} %bitcast.33), channel_id=1, source_target_pairs={{0,1},{1,2},{2,3},{3,4},{4,5},{5,6},{6,7},{7,0},{8,9},{9,10},{10,1... | collective-permute-start | bytes 393224 | tf_op jit(solution)/shard_map/ppermute | solution.py:217
  19.9 8.6 %copy-start = (bf16[2,256,128]{2,1,0:T(8,128)(2,1)}, bf16[2,256,128]{2,1,0:T(8,128)(2,1)S(1)}, u32[]{:S(2)}) copy-start(bf16[2,256,128]{2,1,0:T(8,128)(2,1)S(1)} %collective-permute-done.xlo) | copy-start | bytes 393220
  19.9 8.6 %collective-permute-start.5 = (bf16[16,32,128]{2,1,0:T(8,128)(2,1)S(1)}, bf16[16,32,128]{2,1,0:T(8,128)(2,1)S(1)}, u32[]{:S(2)}, u32[]{:S(2)}) collective-permute-start(bf16[16,32,128]{2,1,0:T(8,128)(2,1)S(1)} %bitcast.31), channel_id=1, source_target_pairs={{1,0},{2,1},{3,2},{4,3},{5,4},{6,5},{7,6},{0,7},{9,8},{10,9},{11,1... | collective-permute-start | bytes 393224 | tf_op jit(solution)/shard_map/ppermute | solution.py:218
  28.2 0.7 copy-start.1
  28.3 0.7 copy-start.2
  28.3 0.7 copy-start.3
  28.3 0.7 copy-start.4
  28.5 0.7 copy-start.5

commit v2 on v1

--- a/solution.py
+++ b/solution.py
@@ -9,13 +9,14 @@
 from jax.sharding import Mesh
 from jax.sharding import PartitionSpec as P
 
-GX = ("gx",)
+GX = ("gx_0", "gx_1")
 GY = ("gy_0", "gy_1")
-GZ = ("gz",)
-NEAR = ("gy_0", "gz")
-FAR = ("gx", "gy_1")
+GZ = ("gz_0", "gz_1")
+NEAR = ("gy_0", "gy_1", "gx_1", "gz_1")
+FAR = ("gx_0", "gz_0")
 HIGHEST = lax.Precision.HIGHEST
 CHUNKS = 4
+VMEM_LIMIT = 24 * 2**20
 
 
 def plane_weights(cy, cz):
@@ -55,30 +56,42 @@
     return lax.broadcasted_iota(jnp.int32, shape, 0), lax.broadcasted_iota(jnp.int32, shape, 1)
 
 
-def apply_kernel(p, xlo, xhi, ylo, yhi, zlo, zhi, pot, weights, high, low, sums):
+def apply_kernel(p, xlo, xhi, ylo, yhi, zlo, zhi, pot, weights, high, low, sums, total):
     cx, cells, bands = p.shape
-    stencil = weights[...]
-    total = None
-    for x in range(cx):
-        def plane(at):
-            ref, at = (xlo, at + 2) if at < 0 else (xhi, at - cx) if at >= cx else (p, at)
-            return ref[at].astype(jnp.float32)
-
+    cy, cz = pot.shape[1:]
+    b = bands
+
+    def plane(at):
+        if isinstance(at, int) and not 0 <= at < cx:
+            return (xlo[at + 2] if at < 0 else xhi[at - cx]).astype(jnp.float32)
+        return p[at].astype(jnp.float32)
+
+    def slab(x):
         own = p[x]
         around = jnp.concatenate([own, ylo[x], yhi[x], zlo[x], zhi[x]], axis=0)
-        kinetic = jnp.dot(stencil, around, preferred_element_type=jnp.float32)
+        kinetic = jnp.dot(weights[...], around, preferred_element_type=jnp.float32)
         kinetic = kinetic + (plane(x - 2) + plane(x + 2)) - 16.0 * (plane(x - 1) + plane(x + 1))
-        given = own.astype(jnp.float32)
-        applied = kinetic * (1.0 / 24.0) + pot[:, x : x + 1] * given
+        lines = pot[x].T
+        given = jnp.concatenate(
+            [jnp.broadcast_to(lines[:, y : y + 1], (cz, b)) for y in range(cy)], axis=0
+        ) * own.astype(jnp.float32)
+        applied = kinetic * (1.0 / 24.0) + given
         top = applied.astype(jnp.bfloat16)
         rest = (applied - top.astype(jnp.float32)).astype(jnp.bfloat16)
         high[x] = top
         low[x] = rest
-        part = over_cells(
+        return over_cells(
             jnp.concatenate([own, top], axis=1), jnp.concatenate([own, top, rest], axis=1)
         )
-        total = part if total is None else total + part
-    b = bands
+
+    total[...] = slab(0) + slab(1) + slab(cx - 2) + slab(cx - 1)
+
+    def two_more(i, carry):
+        x = 2 + 2 * i
+        total[...] += slab(x) + slab(x + 1)
+        return carry
+
+    lax.fori_loop(0, (cx - 4) // 2, two_more, 0)
     row, column = iotas(b, b)
     gram = total[:b, :b]
     cross = total[:b, b : 2 * b] + total[:b, 2 * b :]
@@ -171,8 +184,8 @@
     quotient = diagonal(cross)
     squares = diagonal(square) - quotient * quotient * (2.0 - diagonal(gram))
     norm = jnp.sqrt(jnp.maximum(squares, 0.0) + 1e-06)
-    quotients[...] = jnp.broadcast_to(quotient, (bands, bands)).T[:8]
-    norms[...] = jnp.broadcast_to(norm, (bands, bands)).T[:8]
+    quotients[...] = jnp.broadcast_to(quotient, (bands, bands)).T[:1]
+    norms[...] = jnp.broadcast_to(norm, (bands, bands)).T[:1]
 
     turned = inverse.T
     shifted = (-quotient * inverse).T
@@ -206,6 +219,10 @@
         copy.wait()
 
 
+def near(value):
+    return pltpu.with_memory_space_constraint(value, pltpu.VMEM)
+
+
 def vmem(count):
     return [pl.BlockSpec(memory_space=pltpu.VMEM)] * count
 
@@ -255,14 +272,16 @@
     high, low, sums = pl.pallas_call(
         apply_kernel,
         out_shape=(
-            jax.ShapeDtypeStruct(shape, jnp.bfloat16),
-            jax.ShapeDtypeStruct(shape, jnp.bfloat16),
-            jax.ShapeDtypeStruct((2 * bands, bands), jnp.float32),
+            pltpu.VMEM(shape, jnp.bfloat16),
+            pltpu.VMEM(shape, jnp.bfloat16),
+            pltpu.VMEM((2 * bands, bands), jnp.float32),
         ),
         in_specs=vmem(9),
         out_specs=tuple(vmem(3)),
+        scratch_shapes=[pltpu.VMEM((2 * bands, 3 * bands), jnp.float32)],
+        compiler_params=pltpu.CompilerParams(vmem_limit_bytes=VMEM_LIMIT),
         name="apply",
-    )(planes, xlo, xhi, ylo, yhi, zlo, zhi, potential.reshape(cx, cy * cz).T, weights)
+    )(*map(near, (planes, xlo, xhi, ylo, yhi, zlo, zhi, potential, weights)))
     sums = sum_everywhere(sums)
     flat = (cells, bands)
     kept = pl.BlockSpec(memory_space=pl.ANY)
@@ -271,8 +290,8 @@
         out_shape=(
             jax.ShapeDtypeStruct(flat, jnp.float32),
             jax.ShapeDtypeStruct(flat, jnp.bfloat16),
-            jax.ShapeDtypeStruct((8, bands), jnp.float32),
-            jax.ShapeDtypeStruct((8, bands), jnp.float32),
+            jax.ShapeDtypeStruct((1, bands), jnp.float32),
+            jax.ShapeDtypeStruct((1, bands), jnp.float32),
         ),
         in_specs=vmem(4),
         out_specs=(kept, kept, *vmem(2)),
@@ -283,20 +302,23 @@
             pltpu.VMEM(flat, jnp.bfloat16),
             pltpu.SemaphoreType.DMA((CHUNKS, 2)),
         ],
+        compiler_params=pltpu.CompilerParams(vmem_limit_bytes=VMEM_LIMIT),
         name="finish",
-    )(sums, planes.reshape(flat), high.reshape(flat), low.reshape(flat))
+    )(*map(near, (sums, planes.reshape(flat), high.reshape(flat), low.reshape(flat))))
     whole = (cx, cy, cz, bands)
     return rotated.reshape(whole), residual.reshape(whole), quotients[0], norms[0]
 
 
 def solution(mesh):
+    count = mesh.shape
     torus = Mesh(
-        mesh.devices.reshape(mesh.shape["gx"], 4, 2, mesh.shape["gz"]), ("gx", "gy_0", "gy_1", "gz")
+        mesh.devices.reshape(count["gx"] // 2, 2, count["gy"] // 2, 2, count["gz"] // 2, 2),
+        GX + GY + GZ,
     )
     return jax.shard_map(
         local,
         mesh=torus,
-        in_specs=(P("gx", GY, "gz", None), P("gx", GY, "gz")),
-        out_specs=(P("gx", GY, "gz", None), P("gx", GY, "gz", None), P(), P()),
+        in_specs=(P(GX, GY, GZ, None), P(GX, GY, GZ)),
+        out_specs=(P(GX, GY, GZ, None), P(GX, GY, GZ, None), P(), P()),
         check_vma=False,
     )

time: 96.1 us -> 90.4 us (0.941)
  Pallas kernels: 17.7 us -> 13 us
  waiting for transfers between devices: 0.21 us -> 1.9 us
  local copies, waits for them, and re-layouts: 6.95 us -> 5.33 us
    pallas_call x1, Pallas kernels: 7.26 us -> 4.6 us  [local(): pl.pallas_call(apply_kernel, out_shape=(pltpu.VMEM(shape, jnp.bfloat16),...]
    pallas_call x1, Pallas kernels: 10.4 us -> 8.44 us  [local(): pl.pallas_call(functools.partial(finish_kernel, total_cells), out_shape=(...]
    ppermute x3, waiting for transfers between devices: 0.2 us -> 1.53 us  [from_neighbours(): lax.ppermute(low_edge, axes, [(b, a) for a, b in up])]
    squeeze x1 -> x0, local copies, waits for them, and re-layouts: 1.2 us -> none  [local(): norms[0]]
    all_to_all x3, blocking collectives: 47.4 us -> 46.5 us  [exchange(): return lax.all_to_all(blocks, axes, split_axis=0, concat_axis=0, tiled=True)]
    unnamed x13 -> x6, local copies, waits for them, and re-layouts: 2.33 us -> 1.84 us
  transfers between devices with their start and end apart: 6 -> 6, of which waited for: 1 -> 2; matrix products, arithmetic and copies ran while one was open for 4% -> 3% of each run, Pallas kernels for 0% -> 0%
where the time goes in v2:
time: 90.4 us; the launch traced here: 90 us
  blocking collectives  46.5 us (51%)
  starting transfers between devices  22.5 us (25%)
  Pallas kernels  13 us (14%)
  local copies, waits for them, and re-layouts  5.33 us (6%)
  waiting for transfers between devices  1.9 us (2%)
    all_to_all x3, blocking collectives, exchange(): return lax.all_to_all(blocks, axes, split_axis=0, concat_axis=0, tiled=True)  46.5 us
    ppermute x3, starting transfers between devices, from_neighbours(): lax.ppermute(low_edge, axes, [(b, a) for a, b in up])  14.5 us
    pallas_call x1, Pallas kernels, local(): pl.pallas_call(functools.partial(finish_kernel, total_cells), out_shape=(...  8.44 us
    ppermute x3, starting transfers between devices, from_neighbours(): lax.ppermute(high_edge, axes, up)  8.01 us
    pallas_call x1, Pallas kernels, local(): pl.pallas_call(apply_kernel, out_shape=(pltpu.VMEM(shape, jnp.bfloat16),...  4.6 us
    unnamed x6, local copies, waits for them, and re-layouts  1.84 us
  transfers between devices with their start and end apart: 6, of which 2 were waited for; matrix products, arithmetic and copies ran while one was open for 3% of the time, Pallas kernels for 0%

profile of v2, /device:TPU:1, one launch (start us, length us, event | category | flops | bytes accessed | tf_op | source)
XLA Modules:
  0.0 90.0 jit_solution(6204047950019125429)
XLA Ops:
  0.6 0.0 copy-start
  0.6 1.1 %fusion.2 = (bf16[2,16,16,128]{3,2,1,0:T(8,128)(2,1)S(1)}, bf16[2,16,16,128]{3,2,1,0:T(8,128)(2,1)S(1)}) fusion(bf16[16,16,16,128]{3,2,1,0:T(8,128)(2,1)} %param.3), kind=kLoop, calls=%fused_computation.2 | loop fusion | bytes 524288 | tf_op jit(solution)/shard_map/slice | solution.py:264
  1.7 4.0 %collective-permute-start = (bf16[2,256,128]{2,1,0:T(8,128)(2,1)S(1)}, bf16[2,256,128]{2,1,0:T(8,128)(2,1)S(1)}, u32[]{:S(2)}, u32[]{:S(2)}) collective-permute-start(bf16[2,256,128]{2,1,0:T(8,128)(2,1)S(1)} %bitcast.25), channel_id=1, source_target_pairs={{0,64},{64,128},{128,192},{192,256},{256,320},{320,384},{384,448},... | collective-permute-start | bytes 393224 | tf_op jit(solution)/shard_map/ppermute | solution.py:234
  5.7 3.8 %collective-permute-start.1 = (bf16[2,256,128]{2,1,0:T(8,128)(2,1)S(1)}, bf16[2,256,128]{2,1,0:T(8,128)(2,1)S(1)}, u32[]{:S(2)}, u32[]{:S(2)}) collective-permute-start(bf16[2,256,128]{2,1,0:T(8,128)(2,1)S(1)} %bitcast.22), channel_id=1, source_target_pairs={{64,0},{128,64},{192,128},{256,192},{320,256},{384,320},{448,384},... | collective-permute-start | bytes 393224 | tf_op jit(solution)/shard_map/ppermute | solution.py:235
  9.6 1.0 %fusion.1 = (bf16[16,2,16,128]{3,2,1,0:T(8,128)(2,1)S(1)}, bf16[16,2,16,128]{3,2,1,0:T(8,128)(2,1)S(1)}) fusion(bf16[16,16,16,128]{3,2,1,0:T(8,128)(2,1)} %param.3), kind=kLoop, calls=%fused_computation.1 | loop fusion | bytes 524288 | tf_op jit(solution)/shard_map/slice | solution.py:260
  10.6 2.1 %collective-permute-start.2 = (bf16[16,32,128]{2,1,0:T(8,128)(2,1)S(1)}, bf16[16,32,128]{2,1,0:T(8,128)(2,1)S(1)}, u32[]{:S(2)}, u32[]{:S(2)}) collective-permute-start(bf16[16,32,128]{2,1,0:T(8,128)(2,1)S(1)} %bitcast.24), channel_id=1, source_target_pairs={{0,8},{8,16},{16,24},{24,32},{32,40},{40,48},{48,56},{56,0},{1,9},... | collective-permute-start | bytes 393224 | tf_op jit(solution)/shard_map/ppermute | solution.py:234
  12.6 4.0 %collective-permute-start.3 = (bf16[16,32,128]{2,1,0:T(8,128)(2,1)S(1)}, bf16[16,32,128]{2,1,0:T(8,128)(2,1)S(1)}, u32[]{:S(2)}, u32[]{:S(2)}) collective-permute-start(bf16[16,32,128]{2,1,0:T(8,128)(2,1)S(1)} %bitcast.23), channel_id=1, source_target_pairs={{8,0},{16,8},{24,16},{32,24},{40,32},{48,40},{56,48},{0,56},{9,1},... | collective-permute-start | bytes 393224 | tf_op jit(solution)/shard_map/ppermute | solution.py:235
  16.7 1.4 %fusion = (bf16[16,16,2,128]{3,2,1,0:T(2,128)(2,1)S(1)}, bf16[16,16,2,128]{3,2,1,0:T(2,128)(2,1)S(1)}) fusion(bf16[16,16,16,128]{3,2,1,0:T(8,128)(2,1)} %param.3), kind=kLoop, calls=%fused_computation | loop fusion | bytes 524288 | tf_op jit(solution)/shard_map/slice | solution.py:266
  18.1 1.9 %collective-permute-start.4 = (bf16[16,32,128]{2,1,0:T(8,128)(2,1)S(1)}, bf16[16,32,128]{2,1,0:T(8,128)(2,1)S(1)}, u32[]{:S(2)}, u32[]{:S(2)}) collective-permute-start(bf16[16,32,128]{2,1,0:T(8,128)(2,1)S(1)} %bitcast.27), channel_id=1, source_target_pairs={{0,1},{1,2},{2,3},{3,4},{4,5},{5,6},{6,7},{7,0},{8,9},{9,10},{10,1... | collective-permute-start | bytes 393224 | tf_op jit(solution)/shard_map/ppermute | solution.py:234
  20.0 0.0 collective-permute-done.xlo
  20.0 6.6 %collective-permute-start.5 = (bf16[16,32,128]{2,1,0:T(8,128)(2,1)S(1)}, bf16[16,32,128]{2,1,0:T(8,128)(2,1)S(1)}, u32[]{:S(2)}, u32[]{:S(2)}) collective-permute-start(bf16[16,32,128]{2,1,0:T(8,128)(2,1)S(1)} %bitcast.26), channel_id=1, source_target_pairs={{1,0},{2,1},{3,2},{4,3},{5,4},{6,5},{7,6},{0,7},{9,8},{10,9},{11,1... | collective-permute-start | bytes 393224 | tf_op jit(solution)/shard_map/ppermute | solution.py:235
  26.7 0.0 collective-permute-done.1.xhi
  26.7 0.0 collective-permute-done.2.ylo
  26.7 0.0 collective-permute-done.3.yhi
  26.7 0.4 collective-permute-done.4.zlo
  27.1 1.5 %collective-permute-done.5.zhi = bf16[16,32,128]{2,1,0:T(8,128)(2,1)S(1)} collective-permute-done((bf16[16,32,128]{2,1,0:T(8,128)(2,1)S(1)}, bf16[16,32,128]{2,1,0:T(8,128)(2,1)S(1)}, u32[]{:S(2)}, u32[]{:S(2)}) %collective-permute-start.5) | collective-permute-done | bytes 131104 | tf_op jit(solution)/shard_map/ppermute | solution.py:235
  28.6 0.0 copy-done
  28.6 0.0 copy-start.1
  28.6 0.9 %copy-done.1 = bf16[256,384]{1,0:T(8,128)(2,1)S(1)} copy-done((bf16[256,384]{1,0:T(8,128)(2,1)S(1)}, bf16[256,384]{1,0:T(8,128)(2,1)}, u32[]{:S(2)}) %copy-start.1) | copy-done | bytes 196632
  29.5 0.0 copy-start.2
  29.5 0.9 %copy-done.2 = f32[16,16,16]{2,1,0:T(8,128)S(1)} copy-done((f32[16,16,16]{2,1,0:T(8,128)S(1)}, f32[16,16,16]{2,1,0:T(8,128)}, u32[]{:S(2)}) %copy-start.2) | copy-done | bytes 16408
  30.4 4.6 %apply.1 = (bf16[16,256,128]{2,1,0:T(8,128)(2,1)S(1)}, bf16[16,256,128]{2,1,0:T(8,128)(2,1)S(1)}, f32[256,128]{1,0:T(8,128)S(1)}) custom-call(bf16[16,256,128]{2,1,0:T(8,128)(2,1)S(1)} %bitcast.16, bf16[2,256,128]{2,1,0:T(8,128)(2,1)S(1)} %collective-permute-done.xlo, bf16[2,256,128]{2,1,0:T(8,128)(2,1)S(1)} %collective-permute-done.1.xhi, ...), custom_call_target="tpu_custom_call" | custom-call | tf_op jit(solution)/shard_map/apply/pallas_call | solution.py:272
  35.0 12.5 %all_to_all.15 = f32[32,8,128]{2,1,0:T(8,128)S(1)} all-to-all(f32[32,8,128]{2,1,0:T(8,128)S(1)} %bitcast.21), channel_id=1, replica_groups=mesh['gx_0'=4,'gx_1'=2,'gy_0'=4,'gy_1'=2,'gz_0'=4,'gz_1'=2] {'gy_0','gy_..., dimensions={0} | all-to-all | bytes 262144 | tf_op jit(solution)/shard_map/all_to_all | solution.py:240
  47.6 22.1 %all_to_all.16 = f32[16,8,128]{2,1,0:T(8,128)S(1)} all-to-all(f32[16,8,128]{2,1,0:T(8,128)S(1)} %broadcast_in_dim.6), channel_id=1, replica_groups=mesh['gx_0'=4,'gx_1'=2,'gy_0'=4,'gy_1'=2,'gz_0'=4,'gz_1'=2] {'gx_0','gz_0'}, dimensions={0} | all-to-all | bytes 131072 | tf_op jit(solution)/shard_map/all_to_all | solution.py:240
  69.7 11.8 %all_to_all.17 = f32[32,8,128]{2,1,0:T(8,128)S(1)} all-to-all(f32[32,8,128]{2,1,0:T(8,128)S(1)} %broadcast_in_dim.7), channel_id=1, replica_groups=mesh['gx_0'=4,'gx_1'=2,'gy_0'=4,'gy_1'=2,'gz_0'=4,'gz_1'=2] {'gy_0','gy_..., dimensions={0} | all-to-all | bytes 262144 | tf_op jit(solution)/shard_map/all_to_all | solution.py:240
  81.6 8.4 %finish.1 = (f32[4096,128]{1,0:T(8,128)}, bf16[4096,128]{1,0:T(8,128)(2,1)}, f32[1,128]{1,0:T(1,128)}, f32[1,128]{1,0:T(1,128)}) custom-call(f32[256,128]{1,0:T(8,128)S(1)} %bitcast.20, bf16[4096,128]{1,0:T(8,128)(2,1)S(1)} %bitcast.17, bf16[4096,128]{1,0:T(8,128)(2,1)S(1)} %bitcast.18, bf16[4096,128]{1,0:T(8,128)(2,1)S(1)} %bitcast.19), custom_call_target="tpu_custom_call" | custom-call | tf_op jit(solution)/shard_map/finish/pallas_call | solution.py:288
  (4 shorter events, 0.1 us)
Async XLA Ops:
  0.6 28.0 %copy-start = (bf16[16,16,16,128]{3,2,1,0:T(8,128)(2,1)S(1)}, bf16[16,16,16,128]{3,2,1,0:T(8,128)(2,1)}, u32[]{:S(2)}) copy-start(bf16[16,16,16,128]{3,2,1,0:T(8,128)(2,1)} %param.3) | copy-start | bytes 3145732
  1.7 18.3 %collective-permute-start = (bf16[2,256,128]{2,1,0:T(8,128)(2,1)S(1)}, bf16[2,256,128]{2,1,0:T(8,128)(2,1)S(1)}, u32[]{:S(2)}, u32[]{:S(2)}) collective-permute-start(bf16[2,256,128]{2,1,0:T(8,128)(2,1)S(1)} %bitcast.25), channel_id=1, source_target_pairs={{0,64},{64,128},{128,192},{192,256},{256,320},{320,384},{384,448},... | collective-permute-start | bytes 393224 | tf_op jit(solution)/shard_map/ppermute | solution.py:234
  5.7 20.9 %collective-permute-start.1 = (bf16[2,256,128]{2,1,0:T(8,128)(2,1)S(1)}, bf16[2,256,128]{2,1,0:T(8,128)(2,1)S(1)}, u32[]{:S(2)}, u32[]{:S(2)}) collective-permute-start(bf16[2,256,128]{2,1,0:T(8,128)(2,1)S(1)} %bitcast.22), channel_id=1, source_target_pairs={{64,0},{128,64},{192,128},{256,192},{320,256},{384,320},{448,384},... | collective-permute-start | bytes 393224 | tf_op jit(solution)/shard_map/ppermute | solution.py:235
  10.6 16.1 %collective-permute-start.2 = (bf16[16,32,128]{2,1,0:T(8,128)(2,1)S(1)}, bf16[16,32,128]{2,1,0:T(8,128)(2,1)S(1)}, u32[]{:S(2)}, u32[]{:S(2)}) collective-permute-start(bf16[16,32,128]{2,1,0:T(8,128)(2,1)S(1)} %bitcast.24), channel_id=1, source_target_pairs={{0,8},{8,16},{16,24},{24,32},{32,40},{40,48},{48,56},{56,0},{1,9},... | collective-permute-start | bytes 393224 | tf_op jit(solution)/shard_map/ppermute | solution.py:234
  12.6 14.1 %collective-permute-start.3 = (bf16[16,32,128]{2,1,0:T(8,128)(2,1)S(1)}, bf16[16,32,128]{2,1,0:T(8,128)(2,1)S(1)}, u32[]{:S(2)}, u32[]{:S(2)}) collective-permute-start(bf16[16,32,128]{2,1,0:T(8,128)(2,1)S(1)} %bitcast.23), channel_id=1, source_target_pairs={{8,0},{16,8},{24,16},{32,24},{40,32},{48,40},{56,48},{0,56},{9,1},... | collective-permute-start | bytes 393224 | tf_op jit(solution)/shard_map/ppermute | solution.py:235
  18.1 9.0 %collective-permute-start.4 = (bf16[16,32,128]{2,1,0:T(8,128)(2,1)S(1)}, bf16[16,32,128]{2,1,0:T(8,128)(2,1)S(1)}, u32[]{:S(2)}, u32[]{:S(2)}) collective-permute-start(bf16[16,32,128]{2,1,0:T(8,128)(2,1)S(1)} %bitcast.27), channel_id=1, source_target_pairs={{0,1},{1,2},{2,3},{3,4},{4,5},{5,6},{6,7},{7,0},{8,9},{9,10},{10,1... | collective-permute-start | bytes 393224 | tf_op jit(solution)/shard_map/ppermute | solution.py:234
  20.0 8.6 %collective-permute-start.5 = (bf16[16,32,128]{2,1,0:T(8,128)(2,1)S(1)}, bf16[16,32,128]{2,1,0:T(8,128)(2,1)S(1)}, u32[]{:S(2)}, u32[]{:S(2)}) collective-permute-start(bf16[16,32,128]{2,1,0:T(8,128)(2,1)S(1)} %bitcast.26), channel_id=1, source_target_pairs={{1,0},{2,1},{3,2},{4,3},{5,4},{6,5},{7,6},{0,7},{9,8},{10,9},{11,1... | collective-permute-start | bytes 393224 | tf_op jit(solution)/shard_map/ppermute | solution.py:235
  28.6 0.9 %copy-start.1 = (bf16[256,384]{1,0:T(8,128)(2,1)S(1)}, bf16[256,384]{1,0:T(8,128)(2,1)}, u32[]{:S(2)}) copy-start(bf16[256,384]{1,0:T(8,128)(2,1)} %constant.4.clone.weights) | copy-start | bytes 589828
  29.5 0.9 %copy-start.2 = (f32[16,16,16]{2,1,0:T(8,128)S(1)}, f32[16,16,16]{2,1,0:T(8,128)}, u32[]{:S(2)}) copy-start(f32[16,16,16]{2,1,0:T(8,128)} %pot.1) | copy-start | bytes 49156

commit v3 on v2

v3 whole, which is shorter than its diff:
```python
import functools

import jax
import jax.numpy as jnp
import numpy as np
from jax import lax
from jax.experimental import pallas as pl
from jax.experimental.pallas import tpu as pltpu
from jax.sharding import Mesh
from jax.sharding import PartitionSpec as P

GX = ("gx_0", "gx_1")
GY = ("gy_0", "gy_1")
GZ = ("gz_0", "gz_1")
NEAR = ("gy_0", "gy_1", "gx_1", "gz_1")
FAR = ("gx_0", "gz_0")
HIGHEST = lax.Precision.HIGHEST
CHUNKS = 4
VMEM_LIMIT = 24 * 2**20


def plane_weights(cy, cz):
    side = {0: 90.0, 1: -16.0, 2: 1.0}
    weights = np.zeros((cy * cz, cy * cz + 4 * cz + 4 * cy), np.float32)
    for y in range(cy):
        for z in range(cz):
            row = y * cz + z
            weights[row, row] = side[0]
            for step in (-2, -1, 1, 2):
                w = side[abs(step)]
                base = cy * cz
                if 0 <= y + step < cy:
                    weights[row, row + step * cz] = w
                elif y + step < 0:
                    weights[row, base + (y + step + 2) * cz + z] = w
                else:
                    weights[row, base + 2 * cz + (y + step - cy) * cz + z] = w
                base = cy * cz + 4 * cz
                if 0 <= z + step < cz:
                    weights[row, row + step] = w
                elif z + step < 0:
                    weights[row, base + y * 2 + z + step + 2] = w
                else:
                    weights[row, base + 2 * cy + y * 2 + z + step - cz] = w
    return weights


def over_cells(left, right):
    return lax.dot_general(
        left, right, (((0,), (0,)), ((), ())), preferred_element_type=jnp.float32
    )


def iotas(rows, columns):
    shape = (rows, columns)
    return lax.broadcasted_iota(jnp.int32, shape, 0), lax.broadcasted_iota(jnp.int32, shape, 1)


def prepare_kernel(cy, given, potential, weights, p, xlo, xhi, ylo, yhi, zlo, zhi, pot, w, sems):
    cx, cells, bands = p.shape
    cz = cells // cy
    edge = 2 * cz
    pairs = (
        (given, p),
        (given.at[:2], xlo),
        (given.at[cx - 2 :], xhi),
        (given.at[:, :edge], ylo),
        (given.at[:, cells - edge :], yhi),
        (potential, pot),
        (weights, w),
    )
    copies = [pltpu.make_async_copy(*pair, sems.at[at]) for at, pair in enumerate(pairs)]
    for copy in copies:
        copy.start()
    row, column = iotas(4 * cy, cells)
    side, row = row // (2 * cy), row % (2 * cy)
    source = (row // 2) * cz + row % 2 + side * (cz - 2)
    choice = jnp.where(column == source, 1.0, 0.0).astype(jnp.bfloat16)
    copies[0].wait()
    for x in range(cx):
        faces = jnp.dot(choice, p[x], preferred_element_type=jnp.float32).astype(jnp.bfloat16)
        zlo[x] = faces[: 2 * cy]
        zhi[x] = faces[2 * cy :]
    for copy in copies[1:]:
        copy.wait()


def inner_kernel(p, pot, weights, inner):
    cx, cells, bands = p.shape
    cy, cz = pot.shape[1:]

    def slab(x, steps):
        own = p[x]
        total = jnp.dot(weights[:, :cells], own, preferred_element_type=jnp.float32)
        for step in steps:
            near_by = p[x + step].astype(jnp.float32)
            total = total + near_by if abs(step) == 2 else total - 16.0 * near_by
        lines = pot[x].T
        given = jnp.concatenate(
            [jnp.broadcast_to(lines[:, y : y + 1], (cz, bands)) for y in range(cy)], axis=0
        ) * own.astype(jnp.float32)
        inner[x] = total * (1.0 / 24.0) + given

    for x in range(cx):
        slab(x, [step for step in (-2, -1, 1, 2) if 0 <= x + step < cx])


def apply_kernel(p, inner, xlo, xhi, ylo, yhi, zlo, zhi, weights, high, low, sums):
    cx, cells, bands = p.shape
    b = bands

    def slab(x, outside=()):
        around = jnp.concatenate([ylo[x], yhi[x], zlo[x], zhi[x]], axis=0)
        missing = jnp.dot(weights[:, cells:], around, preferred_element_type=jnp.float32)
        for weight, ref, at in outside:
            missing = missing + weight * ref[at].astype(jnp.float32)
        applied = inner[x] + missing * (1.0 / 24.0)
        top = applied.astype(jnp.bfloat16)
        rest = (applied - top.astype(jnp.float32)).astype(jnp.bfloat16)
        high[x] = top
        low[x] = rest

    outside = {
        0: ((1.0, xlo, 0), (-16.0, xlo, 1)),
        1: ((1.0, xlo, 1),),
        cx - 2: ((1.0, xhi, 0),),
        cx - 1: ((-16.0, xhi, 0), (1.0, xhi, 1)),
    }
    for x in range(cx):
        slab(x, outside.get(x, ()))
    flat = [ref[...].reshape(cx * cells, b) for ref in (p, high, low)]
    total = over_cells(jnp.concatenate(flat[:2], axis=1), jnp.concatenate(flat, axis=1))
    row, column = iotas(b, b)
    gram = total[:b, :b]
    cross = total[:b, b : 2 * b] + total[:b, 2 * b :]
    rest = total[b:, 2 * b :]
    square = total[b:, b : 2 * b] + rest + rest.T
    cross_own = jnp.sum(jnp.where(row == column, cross, 0.0), axis=0, keepdims=True)
    cross = cross + cross.T
    sums[:b] = jnp.where(row >= column, gram, cross)
    spare = jnp.where(row == 0, cross_own, pltpu.roll(jnp.broadcast_to(cross_own, (b, b)), b - 1, 1))
    sums[b:] = jnp.where(row > column, 2.0 * square, jnp.where(row == column, square, spare))


def across(value, lane):
    return jnp.take_along_axis(value, jnp.full(value.shape, lane, jnp.int32), axis=1)


def down(value, row):
    return jnp.broadcast_to(value[row : row + 1, :], value.shape)


def inverse_factor(rows):
    count = len(rows)
    size, bands = rows[0].shape
    row, column = iotas(size, bands)
    rows = list(rows)
    right = [jnp.where(column == row + size * k, 1.0, 0.0) for k in range(count)]
    done = []
    for k in range(count):
        lines = {i: [] for i in range(k, count)}
        for c in range(size):
            for i in range(k, count):
                lines[i].append(across(rows[i], size * k + c))
        own = lines.pop(k) + [rows[k], right[k]]
        result = jnp.zeros_like(right[k])
        for c in range(size):
            here = row == c
            pivot = down(own[c], c)
            scale = lax.rsqrt(pivot)
            share = 1.0 / pivot
            factor = jnp.where(here, -1.0, own[c])
            result = jnp.where(here, own[-1] * scale, result)
            for d in range(c + 1, len(own)):
                own[d] = jnp.where(here, 0.0, own[d]) - factor * (down(own[d], c) * share)
        done.append(result)
        heads = [(down(own[-2], c), down(own[-1], c)) for c in range(size)]
        for i, line in lines.items():
            for at, (left_row, right_row) in zip(line, heads):
                rows[i] = rows[i] - at * left_row
                right[i] = right[i] - at * right_row
    return done


def split_3(value):
    parts = []
    for _ in range(3):
        part = value.astype(jnp.bfloat16)
        value = value - part.astype(jnp.float32)
        parts.append(part)
    return parts


def finish_kernel(
    cells, sums, p, high, low, rotated, residual, quotients, norms, w, out_r, out_s, sems
):
    rows, bands = p.shape
    row, column = iotas(bands, bands)
    scale = 1.0 / cells
    first, second = sums[:bands] * scale, sums[bands:] * scale
    lower = jnp.where(row >= column, first, 0.0)
    gram = lower + jnp.where(row > column, first, 0.0).T
    own = jnp.where(column[:1] == 0, pltpu.roll(second[:8], 1, 1)[1:2], second[:1])
    cross = jnp.where(row < column, first, jnp.where(row == column, own, 0.0))
    square = jnp.where(row >= column, second, 0.0)
    size = 8
    inverse = jnp.concatenate(
        inverse_factor([gram[i : i + size] for i in range(0, bands, size)]), axis=0
    )

    def diagonal(matrix):
        product = jnp.dot(inverse, matrix, precision=HIGHEST, preferred_element_type=jnp.float32)
        return jnp.sum(product * inverse, axis=1, keepdims=True)

    quotient = diagonal(cross)
    squares = diagonal(square) - quotient * quotient * (2.0 - diagonal(gram))
    norm = jnp.sqrt(jnp.maximum(squares, 0.0) + 1e-06)
    quotients[...] = jnp.broadcast_to(quotient, (bands, bands)).T[:1]
    norms[...] = jnp.broadcast_to(norm, (bands, bands)).T[:1]

    turned = inverse.T
    shifted = (-quotient * inverse).T
    none = jnp.zeros((bands, bands), jnp.bfloat16)
    for at, (a, s) in enumerate(zip(split_3(turned), split_3(shifted))):
        w[at, :bands, :bands] = a
        w[at, :bands, bands:] = s
        w[at, bands:, :bands] = none
        w[at, bands:, bands:] = a if at < 2 else w[0, bands:, bands:]
    step = rows // CHUNKS
    copies = []
    for chunk in range(CHUNKS):
        part = pl.ds(chunk * step, step)
        both = jnp.concatenate([p[part], high[part]], axis=1)
        rest = jnp.concatenate([p[part], low[part]], axis=1)
        result = jnp.dot(rest, w[2], preferred_element_type=jnp.float32)
        result = result + jnp.dot(both, w[1], preferred_element_type=jnp.float32)
        result = result + jnp.dot(both, w[0], preferred_element_type=jnp.float32)
        out_r[part] = result[:, :bands]
        out_s[part] = result[:, bands:].astype(jnp.bfloat16)
        for at, (source, target) in enumerate(((out_r, rotated), (out_s, residual))):
            copy = pltpu.make_async_copy(source.at[part], target.at[part], sems.at[chunk, at])
            copy.start()
            copies.append(copy)
    for copy in copies:
        copy.wait()


def near(value):
    return pltpu.with_memory_space_constraint(value, pltpu.VMEM)


def far(value):
    return pltpu.with_memory_space_constraint(value, pltpu.HBM)


def from_neighbours(low_edge, high_edge, axes):
    count = lax.axis_size(axes)
    up = [(i, (i + 1) % count) for i in range(count)]
    return (
        lax.ppermute(high_edge, axes, up),
        lax.ppermute(low_edge, axes, [(b, a) for a, b in up]),
    )


def kernel_call(kernel, outs, ins, outs_at, scratch=(), **kept):
    return pl.pallas_call(
        kernel,
        out_shape=outs,
        in_specs=[pl.BlockSpec(memory_space=space) for space in ins],
        out_specs=tuple(pl.BlockSpec(memory_space=space) for space in outs_at),
        scratch_shapes=scratch,
        compiler_params=pltpu.CompilerParams(vmem_limit_bytes=VMEM_LIMIT),
        **kept,
    )


def exchange(blocks, axes):
    return lax.all_to_all(blocks, axes, split_axis=0, concat_axis=0, tiled=True)


def for_each(value, axes):
    return exchange(jnp.broadcast_to(value, (lax.axis_size(axes), *value.shape)), axes)


def sum_everywhere(value):
    rows, columns = value.shape
    own = jnp.sum(exchange(value.reshape(lax.axis_size(NEAR), -1, columns), NEAR), axis=0)
    own = jnp.sum(for_each(own, FAR), axis=0)
    return for_each(own, NEAR).reshape(rows, columns)


def local(wavefunctions, potential):
    cx, cy, cz, bands = wavefunctions.shape
    cells = cx * cy * cz
    total_cells = cells * lax.axis_size(GX) * lax.axis_size(GY) * lax.axis_size(GZ)
    planes = wavefunctions.reshape(cx, cy * cz, bands)
    weights = jnp.asarray(plane_weights(cy, cz), jnp.bfloat16)
    shape = planes.shape
    on_chip, off_chip = pltpu.VMEM, pltpu.HBM

    def half(*dims):
        return on_chip(dims, jnp.bfloat16)

    p, *edges, pot, w = kernel_call(
        functools.partial(prepare_kernel, cy),
        (
            half(*shape),
            *[half(2, cy * cz, bands)] * 2,
            *[half(cx, 2 * cz, bands)] * 2,
            *[half(cx, 2 * cy, bands)] * 2,
            on_chip(potential.shape, jnp.float32),
            half(*weights.shape),
        ),
        [off_chip] * 3,
        [on_chip] * 9,
        [pltpu.SemaphoreType.DMA((7,))],
        name="prepare",
    )(*map(far, (planes, potential, weights)))
    xlo, xhi = from_neighbours(*edges[:2], GX)
    ylo, yhi = from_neighbours(*edges[2:4], GY)
    zlo, zhi = from_neighbours(*edges[4:], GZ)
    inner = kernel_call(
        inner_kernel, (on_chip(shape, jnp.float32),), [on_chip] * 3, [on_chip], name="inner"
    )(*map(near, (p, pot, w)))[0]
    high, low, sums = kernel_call(
        apply_kernel,
        (half(*shape), half(*shape), on_chip((2 * bands, bands), jnp.float32)),
        [on_chip] * 9,
        [on_chip] * 3,
        name="apply",
    )(*map(near, (p, inner, xlo, xhi, ylo, yhi, zlo, zhi, w)))
    sums = sum_everywhere(sums)
    flat = (cells, bands)
    line = jax.ShapeDtypeStruct((1, bands), jnp.float32)
    rotated, residual, quotients, norms = kernel_call(
        functools.partial(finish_kernel, total_cells),
        (
            jax.ShapeDtypeStruct(flat, jnp.float32),
            jax.ShapeDtypeStruct(flat, jnp.bfloat16),
            line,
            line,
        ),
        [on_chip] * 4,
        [off_chip, off_chip, on_chip, on_chip],
        [
            pltpu.VMEM((3, 2 * bands, 2 * bands), jnp.bfloat16),
            pltpu.VMEM(flat, jnp.float32),
            pltpu.VMEM(flat, jnp.bfloat16),
            pltpu.SemaphoreType.DMA((CHUNKS, 2)),
        ],
        name="finish",
    )(*map(near, (sums, p.reshape(flat), high.reshape(flat), low.reshape(flat))))
    whole = (cx, cy, cz, bands)
    return rotated.reshape(whole), residual.reshape(whole), quotients[0], norms[0]


def solution(mesh):
    count = mesh.shape
    torus = Mesh(
        mesh.devices.reshape(count["gx"] // 2, 2, count["gy"] // 2, 2, count["gz"] // 2, 2),
        GX + GY + GZ,
    )
    return jax.shard_map(
        local,
        mesh=torus,
        in_specs=(P(GX, GY, GZ, None), P(GX, GY, GZ)),
        out_specs=(P(GX, GY, GZ, None), P(GX, GY, GZ, None), P(), P()),
        check_vma=False,
    )
```

time: 90.4 us -> 83.1 us (0.919)
  local copies, waits for them, and re-layouts: 5.33 us -> 0.02 us
  waiting for transfers between devices: 1.9 us -> 0.55 us
    slice x3 -> x0, local copies, waits for them, and re-layouts: 3.47 us -> none  [the longest x1 1.41 us: local(): wavefunctions[:, :, :2].reshape(cx, 2 * cy, bands)]
    unnamed x6 -> x0, local copies, waits for them, and re-layouts: 1.84 us -> none
    ppermute x3, waiting for transfers between devices: 1.53 us -> 0.54 us  [from_neighbours(): lax.ppermute(low_edge, axes, [(b, a) for a, b in up])]
    pallas_call x2 -> x4, Pallas kernels: 13 us -> 12.5 us  [the longest x1 7.8 us: local(): kernel_call(functools.partial(finish_kernel, total_cells), (jax.ShapeDtyp...]
  transfers between devices with their start and end apart: 6 -> 6, of which waited for: 2 -> 1; matrix products, arithmetic and copies ran while one was open for 3% -> 0% of each run, Pallas kernels for 0% -> 2%
where the time goes in v3:
time: 83.1 us; the launch traced here: 82.8 us
  blocking collectives  46.5 us (56%)
  starting transfers between devices  22.5 us (27%)
  Pallas kernels  12.5 us (15%)
    all_to_all x3, blocking collectives, exchange(): return lax.all_to_all(blocks, axes, split_axis=0, concat_axis=0, tiled=True)  46.5 us
    ppermute x3, starting transfers between devices, from_neighbours(): lax.ppermute(low_edge, axes, [(b, a) for a, b in up])  14.5 us
    ppermute x3, starting transfers between devices, from_neighbours(): lax.ppermute(high_edge, axes, up)  7.99 us
    pallas_call x1, Pallas kernels, local(): kernel_call(functools.partial(finish_kernel, total_cells), (jax.ShapeDtyp...  7.8 us
    pallas_call x1, Pallas kernels, local(): kernel_call(apply_kernel, (half(*shape), half(*shape), on_chip((2 * bands...  1.72 us
  transfers between devices with their start and end apart: 6, of which 1 were waited for; matrix products, arithmetic and copies ran while one was open for 0% of the time, Pallas kernels for 2%

profile of v3, /device:TPU:1, one launch (start us, length us, event | category | flops | bytes accessed | tf_op | source)
XLA Modules:
  0.0 82.8 jit_solution(12972868742843056457)
XLA Ops:
  0.6 1.6 %prepare.1 = (bf16[16,256,128]{2,1,0:T(8,128)(2,1)S(1)}, bf16[2,256,128]{2,1,0:T(8,128)(2,1)S(1)}, bf16[2,256,128]{2,1,0:T(8,128)(2,1)S(1)}, bf16[16,32,128]{2,1...) custom-call(bf16[16,256,128]{2,1,0:T(8,128)(2,1)} %bitcast.15, ...), custom_call_target="tpu_custom_call" | custom-call | tf_op jit(solution)/shard_map/prepare/pallas_call | solution.py:304
  2.3 4.0 %collective-permute-start = (bf16[2,256,128]{2,1,0:T(8,128)(2,1)S(1)}, bf16[2,256,128]{2,1,0:T(8,128)(2,1)S(1)}, u32[]{:S(2)}, u32[]{:S(2)}) collective-permute-start(bf16[2,256,128]{2,1,0:T(8,128)(2,1)S(1)} %get-tuple-element.23), channel_id=1, source_target_pairs={{0,64},{64,128},{128,192},{192,256},{256,320},{320,384},{384,448},... | collective-permute-start | bytes 393224 | tf_op jit(solution)/shard_map/ppermute | solution.py:260
  6.3 3.8 %collective-permute-start.1 = (bf16[2,256,128]{2,1,0:T(8,128)(2,1)S(1)}, bf16[2,256,128]{2,1,0:T(8,128)(2,1)S(1)}, u32[]{:S(2)}, u32[]{:S(2)}) collective-permute-start(bf16[2,256,128]{2,1,0:T(8,128)(2,1)S(1)} %get-tuple-element.24), channel_id=1, source_target_pairs={{64,0},{128,64},{192,128},{256,192},{320,256},{384,320},{448,384},... | collective-permute-start | bytes 393224 | tf_op jit(solution)/shard_map/ppermute | solution.py:261
  10.1 2.1 %collective-permute-start.2 = (bf16[16,32,128]{2,1,0:T(8,128)(2,1)S(1)}, bf16[16,32,128]{2,1,0:T(8,128)(2,1)S(1)}, u32[]{:S(2)}, u32[]{:S(2)}) collective-permute-start(bf16[16,32,128]{2,1,0:T(8,128)(2,1)S(1)} %get-tuple-element.25), channel_id=1, source_target_pairs={{0,8},{8,16},{16,24},{24,32},{32,40},{40,48},{48,56},{56,0},{1,9},... | collective-permute-start | bytes 393224 | tf_op jit(solution)/shard_map/ppermute | solution.py:260
  12.2 4.0 %collective-permute-start.3 = (bf16[16,32,128]{2,1,0:T(8,128)(2,1)S(1)}, bf16[16,32,128]{2,1,0:T(8,128)(2,1)S(1)}, u32[]{:S(2)}, u32[]{:S(2)}) collective-permute-start(bf16[16,32,128]{2,1,0:T(8,128)(2,1)S(1)} %get-tuple-element.26), channel_id=1, source_target_pairs={{8,0},{16,8},{24,16},{32,24},{40,32},{48,40},{56,48},{0,56},{9,1},... | collective-permute-start | bytes 393224 | tf_op jit(solution)/shard_map/ppermute | solution.py:261
  16.2 1.9 %collective-permute-start.4 = (bf16[16,32,128]{2,1,0:T(8,128)(2,1)S(1)}, bf16[16,32,128]{2,1,0:T(8,128)(2,1)S(1)}, u32[]{:S(2)}, u32[]{:S(2)}) collective-permute-start(bf16[16,32,128]{2,1,0:T(8,128)(2,1)S(1)} %get-tuple-element.27), channel_id=1, source_target_pairs={{0,1},{1,2},{2,3},{3,4},{4,5},{5,6},{6,7},{7,0},{8,9},{9,10},{10,1... | collective-permute-start | bytes 393224 | tf_op jit(solution)/shard_map/ppermute | solution.py:260
  18.1 0.0 collective-permute-done.xlo
  18.1 6.6 %collective-permute-start.5 = (bf16[16,32,128]{2,1,0:T(8,128)(2,1)S(1)}, bf16[16,32,128]{2,1,0:T(8,128)(2,1)S(1)}, u32[]{:S(2)}, u32[]{:S(2)}) collective-permute-start(bf16[16,32,128]{2,1,0:T(8,128)(2,1)S(1)} %get-tuple-element.28), channel_id=1, source_target_pairs={{1,0},{2,1},{3,2},{4,3},{5,4},{6,5},{7,6},{0,7},{9,8},{10,9},{11,1... | collective-permute-start | bytes 393224 | tf_op jit(solution)/shard_map/ppermute | solution.py:261
  24.8 1.3 %inner.1 = f32[16,256,128]{2,1,0:T(8,128)S(1)} custom-call(bf16[16,256,128]{2,1,0:T(8,128)(2,1)S(1)} %get-tuple-element.20.p, f32[16,16,16]{2,1,0:T(8,128)S(1)} %get-tuple-element.21.pot, bf16[256,384]{1,0:T(8,128)(2,1)S(1)} %get-tuple-element.22.weights), custom_call_target="tpu_custom_call" | custom-call | tf_op jit(solution)/shard_map/inner/pallas_call | solution.py:322
  26.1 0.0 collective-permute-done.1.xhi
  26.1 0.0 collective-permute-done.2.ylo
  26.1 0.0 collective-permute-done.3.yhi
  26.2 0.0 collective-permute-done.4.zlo
  26.2 0.5 collective-permute-done.5.zhi
  26.7 1.7 %apply.1 = (bf16[16,256,128]{2,1,0:T(8,128)(2,1)S(1)}, bf16[16,256,128]{2,1,0:T(8,128)(2,1)S(1)}, f32[256,128]{1,0:T(8,128)S(1)}) custom-call(bf16[16,256,128]{2,1,0:T(8,128)(2,1)S(1)} %get-tuple-element.20.p, f32[16,256,128]{2,1,0:T(8,128)S(1)} %inner.1, bf16[2,256,128]{2,1,0:T(8,128)(2,1)S(1)} %collective-permute-done.xlo, ...), custom_call_target="tpu_custom_call" | custom-call | tf_op jit(solution)/shard_map/apply/pallas_call | solution.py:325
  28.4 12.5 %all_to_all.15 = f32[32,8,128]{2,1,0:T(8,128)S(1)} all-to-all(f32[32,8,128]{2,1,0:T(8,128)S(1)} %bitcast.14), channel_id=1, replica_groups=mesh['gx_0'=4,'gx_1'=2,'gy_0'=4,'gy_1'=2,'gz_0'=4,'gz_1'=2] {'gy_0','gy_..., dimensions={0} | all-to-all | bytes 262144 | tf_op jit(solution)/shard_map/all_to_all | solution.py:278
  41.0 22.1 %all_to_all.16 = f32[16,8,128]{2,1,0:T(8,128)S(1)} all-to-all(f32[16,8,128]{2,1,0:T(8,128)S(1)} %broadcast_in_dim.6), channel_id=1, replica_groups=mesh['gx_0'=4,'gx_1'=2,'gy_0'=4,'gy_1'=2,'gz_0'=4,'gz_1'=2] {'gx_0','gz_0'}, dimensions={0} | all-to-all | bytes 131072 | tf_op jit(solution)/shard_map/all_to_all | solution.py:278
  63.2 11.8 %all_to_all.17 = f32[32,8,128]{2,1,0:T(8,128)S(1)} all-to-all(f32[32,8,128]{2,1,0:T(8,128)S(1)} %broadcast_in_dim.7), channel_id=1, replica_groups=mesh['gx_0'=4,'gx_1'=2,'gy_0'=4,'gy_1'=2,'gz_0'=4,'gz_1'=2] {'gy_0','gy_..., dimensions={0} | all-to-all | bytes 262144 | tf_op jit(solution)/shard_map/all_to_all | solution.py:278
  75.0 7.8 %finish.1 = (f32[4096,128]{1,0:T(8,128)}, bf16[4096,128]{1,0:T(8,128)(2,1)}, f32[1,128]{1,0:T(1,128)}, f32[1,128]{1,0:T(1,128)}) custom-call(f32[256,128]{1,0:T(8,128)S(1)} %bitcast.13, bf16[4096,128]{1,0:T(8,128)(2,1)S(1)} %bitcast.10, bf16[4096,128]{1,0:T(8,128)(2,1)S(1)} %bitcast.11, bf16[4096,128]{1,0:T(8,128)(2,1)S(1)} %bitcast.12), custom_call_target="tpu_custom_call" | custom-call | tf_op jit(solution)/shard_map/finish/pallas_call | solution.py:335
  (4 shorter events, 0.1 us)
Async XLA Ops:
  2.3 15.9 %collective-permute-start = (bf16[2,256,128]{2,1,0:T(8,128)(2,1)S(1)}, bf16[2,256,128]{2,1,0:T(8,128)(2,1)S(1)}, u32[]{:S(2)}, u32[]{:S(2)}) collective-permute-start(bf16[2,256,128]{2,1,0:T(8,128)(2,1)S(1)} %get-tuple-element.23), channel_id=1, source_target_pairs={{0,64},{64,128},{128,192},{192,256},{256,320},{320,384},{384,448},... | collective-permute-start | bytes 393224 | tf_op jit(solution)/shard_map/ppermute | solution.py:260
  6.3 19.8 %collective-permute-start.1 = (bf16[2,256,128]{2,1,0:T(8,128)(2,1)S(1)}, bf16[2,256,128]{2,1,0:T(8,128)(2,1)S(1)}, u32[]{:S(2)}, u32[]{:S(2)}) collective-permute-start(bf16[2,256,128]{2,1,0:T(8,128)(2,1)S(1)} %get-tuple-element.24), channel_id=1, source_target_pairs={{64,0},{128,64},{192,128},{256,192},{320,256},{384,320},{448,384},... | collective-permute-start | bytes 393224 | tf_op jit(solution)/shard_map/ppermute | solution.py:261
  10.1 16.0 %collective-permute-start.2 = (bf16[16,32,128]{2,1,0:T(8,128)(2,1)S(1)}, bf16[16,32,128]{2,1,0:T(8,128)(2,1)S(1)}, u32[]{:S(2)}, u32[]{:S(2)}) collective-permute-start(bf16[16,32,128]{2,1,0:T(8,128)(2,1)S(1)} %get-tuple-element.25), channel_id=1, source_target_pairs={{0,8},{8,16},{16,24},{24,32},{32,40},{40,48},{48,56},{56,0},{1,9},... | collective-permute-start | bytes 393224 | tf_op jit(solution)/shard_map/ppermute | solution.py:260
  12.2 14.0 %collective-permute-start.3 = (bf16[16,32,128]{2,1,0:T(8,128)(2,1)S(1)}, bf16[16,32,128]{2,1,0:T(8,128)(2,1)S(1)}, u32[]{:S(2)}, u32[]{:S(2)}) collective-permute-start(bf16[16,32,128]{2,1,0:T(8,128)(2,1)S(1)} %get-tuple-element.26), channel_id=1, source_target_pairs={{8,0},{16,8},{24,16},{32,24},{40,32},{48,40},{56,48},{0,56},{9,1},... | collective-permute-start | bytes 393224 | tf_op jit(solution)/shard_map/ppermute | solution.py:261
  16.2 10.0 %collective-permute-start.4 = (bf16[16,32,128]{2,1,0:T(8,128)(2,1)S(1)}, bf16[16,32,128]{2,1,0:T(8,128)(2,1)S(1)}, u32[]{:S(2)}, u32[]{:S(2)}) collective-permute-start(bf16[16,32,128]{2,1,0:T(8,128)(2,1)S(1)} %get-tuple-element.27), channel_id=1, source_target_pairs={{0,1},{1,2},{2,3},{3,4},{4,5},{5,6},{6,7},{7,0},{8,9},{9,10},{10,1... | collective-permute-start | bytes 393224 | tf_op jit(solution)/shard_map/ppermute | solution.py:260
  18.1 8.6 %collective-permute-start.5 = (bf16[16,32,128]{2,1,0:T(8,128)(2,1)S(1)}, bf16[16,32,128]{2,1,0:T(8,128)(2,1)S(1)}, u32[]{:S(2)}, u32[]{:S(2)}) collective-permute-start(bf16[16,32,128]{2,1,0:T(8,128)(2,1)S(1)} %get-tuple-element.28), channel_id=1, source_target_pairs={{1,0},{2,1},{3,2},{4,3},{5,4},{6,5},{7,6},{0,7},{9,8},{10,9},{11,1... | collective-permute-start | bytes 393224 | tf_op jit(solution)/shard_map/ppermute | solution.py:261

commit v4 on v3

--- a/solution.py
+++ b/solution.py
@@ -15,7 +15,7 @@
 NEAR = ("gy_0", "gy_1", "gx_1", "gz_1")
 FAR = ("gx_0", "gz_0")
 HIGHEST = lax.Precision.HIGHEST
-CHUNKS = 4
+CHUNKS = (512,) * 8
 VMEM_LIMIT = 24 * 2**20
 
 
@@ -105,7 +105,7 @@
         slab(x, [step for step in (-2, -1, 1, 2) if 0 <= x + step < cx])
 
 
-def apply_kernel(p, inner, xlo, xhi, ylo, yhi, zlo, zhi, weights, high, low, sums):
+def apply_kernel(p, inner, ylo, yhi, xlo, zlo, xhi, zhi, weights, high, low, sums):
     cx, cells, bands = p.shape
     b = bands
 
@@ -158,10 +158,9 @@
     right = [jnp.where(column == row + size * k, 1.0, 0.0) for k in range(count)]
     done = []
     for k in range(count):
-        lines = {i: [] for i in range(k, count)}
-        for c in range(size):
-            for i in range(k, count):
-                lines[i].append(across(rows[i], size * k + c))
+        lines = {
+            i: [across(rows[i], size * k + c) for c in range(size)] for i in range(k, count)
+        }
         own = lines.pop(k) + [rows[k], right[k]]
         result = jnp.zeros_like(right[k])
         for c in range(size):
@@ -176,9 +175,9 @@
         done.append(result)
         heads = [(down(own[-2], c), down(own[-1], c)) for c in range(size)]
         for i, line in lines.items():
-            for at, (left_row, right_row) in zip(line, heads):
-                rows[i] = rows[i] - at * left_row
-                right[i] = right[i] - at * right_row
+            for at in range(0, size, 2):
+                rows[i] = rows[i] - (line[at] * heads[at][0] + line[at + 1] * heads[at + 1][0])
+                right[i] = right[i] - (line[at] * heads[at][1] + line[at + 1] * heads[at + 1][1])
     return done
 
 
@@ -194,7 +193,7 @@
 def finish_kernel(
     cells, sums, p, high, low, rotated, residual, quotients, norms, w, out_r, out_s, sems
 ):
-    rows, bands = p.shape
+    bands = p.shape[1]
     row, column = iotas(bands, bands)
     scale = 1.0 / cells
     first, second = sums[:bands] * scale, sums[bands:] * scale
@@ -203,40 +202,38 @@
     own = jnp.where(column[:1] == 0, pltpu.roll(second[:8], 1, 1)[1:2], second[:1])
     cross = jnp.where(row < column, first, jnp.where(row == column, own, 0.0))
     square = jnp.where(row >= column, second, 0.0)
-    size = 8
-    inverse = jnp.concatenate(
+    size = 16
+    turned = jnp.concatenate(
         inverse_factor([gram[i : i + size] for i in range(0, bands, size)]), axis=0
-    )
+    ).T
+    none = jnp.zeros((bands, bands), jnp.bfloat16)
+    for at, part in enumerate(split_3(turned)):
+        w[at, :bands, :bands] = part
+        w[at, :bands, bands:] = none
+        w[at, bands:, :bands] = none
+        w[at, bands:, bands:] = part if at < 2 else w[0, bands:, bands:]
 
     def diagonal(matrix):
-        product = jnp.dot(inverse, matrix, precision=HIGHEST, preferred_element_type=jnp.float32)
-        return jnp.sum(product * inverse, axis=1, keepdims=True)
+        product = jnp.dot(matrix, turned, precision=HIGHEST, preferred_element_type=jnp.float32)
+        return jnp.sum(product * turned, axis=0, keepdims=True)
 
     quotient = diagonal(cross)
     squares = diagonal(square) - quotient * quotient * (2.0 - diagonal(gram))
-    norm = jnp.sqrt(jnp.maximum(squares, 0.0) + 1e-06)
-    quotients[...] = jnp.broadcast_to(quotient, (bands, bands)).T[:1]
-    norms[...] = jnp.broadcast_to(norm, (bands, bands)).T[:1]
-
-    turned = inverse.T
-    shifted = (-quotient * inverse).T
-    none = jnp.zeros((bands, bands), jnp.bfloat16)
-    for at, (a, s) in enumerate(zip(split_3(turned), split_3(shifted))):
-        w[at, :bands, :bands] = a
-        w[at, :bands, bands:] = s
-        w[at, bands:, :bands] = none
-        w[at, bands:, bands:] = a if at < 2 else w[0, bands:, bands:]
-    step = rows // CHUNKS
+    quotients[...] = quotient
+    norms[...] = jnp.sqrt(jnp.maximum(squares, 0.0) + 1e-06)
     copies = []
-    for chunk in range(CHUNKS):
-        part = pl.ds(chunk * step, step)
+    start = 0
+    for chunk, step in enumerate(CHUNKS):
+        part = pl.ds(start, step)
+        start += step
         both = jnp.concatenate([p[part], high[part]], axis=1)
         rest = jnp.concatenate([p[part], low[part]], axis=1)
         result = jnp.dot(rest, w[2], preferred_element_type=jnp.float32)
         result = result + jnp.dot(both, w[1], preferred_element_type=jnp.float32)
         result = result + jnp.dot(both, w[0], preferred_element_type=jnp.float32)
-        out_r[part] = result[:, :bands]
-        out_s[part] = result[:, bands:].astype(jnp.bfloat16)
+        bands_now = result[:, :bands]
+        out_r[part] = bands_now
+        out_s[part] = (result[:, bands:] - quotient * bands_now).astype(jnp.bfloat16)
         for at, (source, target) in enumerate(((out_r, rotated), (out_s, residual))):
             copy = pltpu.make_async_copy(source.at[part], target.at[part], sems.at[chunk, at])
             copy.start()
@@ -253,13 +250,14 @@
     return pltpu.with_memory_space_constraint(value, pltpu.HBM)
 
 
-def from_neighbours(low_edge, high_edge, axes):
+def from_below(edge, axes):
     count = lax.axis_size(axes)
-    up = [(i, (i + 1) % count) for i in range(count)]
-    return (
-        lax.ppermute(high_edge, axes, up),
-        lax.ppermute(low_edge, axes, [(b, a) for a, b in up]),
-    )
+    return lax.ppermute(edge, axes, [(i, (i + 1) % count) for i in range(count)])
+
+
+def from_above(edge, axes):
+    count = lax.axis_size(axes)
+    return lax.ppermute(edge, axes, [((i + 1) % count, i) for i in range(count)])
 
 
 def kernel_call(kernel, outs, ins, outs_at, scratch=(), **kept):
@@ -316,9 +314,10 @@
         [pltpu.SemaphoreType.DMA((7,))],
         name="prepare",
     )(*map(far, (planes, potential, weights)))
-    xlo, xhi = from_neighbours(*edges[:2], GX)
-    ylo, yhi = from_neighbours(*edges[2:4], GY)
-    zlo, zhi = from_neighbours(*edges[4:], GZ)
+    xlow, xhigh, ylow, yhigh, zlow, zhigh = edges
+    ylo, yhi = from_below(yhigh, GY), from_above(ylow, GY)
+    xlo, zlo = from_below(xhigh, GX), from_below(zhigh, GZ)
+    xhi, zhi = from_above(xlow, GX), from_above(zlow, GZ)
     inner = kernel_call(
         inner_kernel, (on_chip(shape, jnp.float32),), [on_chip] * 3, [on_chip], name="inner"
     )(*map(near, (p, pot, w)))[0]
@@ -328,7 +327,7 @@
         [on_chip] * 9,
         [on_chip] * 3,
         name="apply",
-    )(*map(near, (p, inner, xlo, xhi, ylo, yhi, zlo, zhi, w)))
+    )(*map(near, (p, inner, ylo, yhi, xlo, zlo, xhi, zhi, w)))
     sums = sum_everywhere(sums)
     flat = (cells, bands)
     line = jax.ShapeDtypeStruct((1, bands), jnp.float32)
@@ -346,7 +345,7 @@
             pltpu.VMEM((3, 2 * bands, 2 * bands), jnp.bfloat16),
             pltpu.VMEM(flat, jnp.float32),
             pltpu.VMEM(flat, jnp.bfloat16),
-            pltpu.SemaphoreType.DMA((CHUNKS, 2)),
+            pltpu.SemaphoreType.DMA((len(CHUNKS), 2)),
         ],
         name="finish",
     )(*map(near, (sums, p.reshape(flat), high.reshape(flat), low.reshape(flat))))

time: 83.1 us -> 82.1 us (0.988)
  Pallas kernels: 12.5 us -> 11.5 us
    pallas_call x1, Pallas kernels: 7.8 us -> 6.77 us  [local(): kernel_call(functools.partial(finish_kernel, total_cells), (jax.ShapeDtyp...]
where the time goes in v4:
time: 82.1 us; the launch traced here: 81.7 us
  blocking collectives  46.7 us (57%)
  starting transfers between devices  22.2 us (27%)
  Pallas kernels  11.5 us (14%)
    all_to_all x3, blocking collectives, exchange(): return lax.all_to_all(blocks, axes, split_axis=0, concat_axis=0, tiled=True)  46.7 us
    ppermute x3, starting transfers between devices, from_above(): lax.ppermute(edge, axes, [((i + 1) % count, i) for i in range(count)])  15.8 us
    pallas_call x1, Pallas kernels, local(): kernel_call(functools.partial(finish_kernel, total_cells), (jax.ShapeDtyp...  6.77 us
    ppermute x3, starting transfers between devices, from_below(): lax.ppermute(edge, axes, [(i, (i + 1) % count) for i in range(count)])  6.43 us
    pallas_call x1, Pallas kernels, local(): kernel_call(apply_kernel, (half(*shape), half(*shape), on_chip((2 * bands...  1.72 us
  transfers between devices with their start and end apart: 6, of which 1 were waited for; matrix products, arithmetic and copies ran while one was open for 0% of the time, Pallas kernels for 2%

profile of v4, /device:TPU:1, one launch (start us, length us, event | category | flops | bytes accessed | tf_op | source)
XLA Modules:
  0.0 81.7 jit_solution(11498704478936687948)
XLA Ops:
  0.6 1.6 %prepare.1 = (bf16[16,256,128]{2,1,0:T(8,128)(2,1)S(1)}, bf16[2,256,128]{2,1,0:T(8,128)(2,1)S(1)}, bf16[2,256,128]{2,1,0:T(8,128)(2,1)S(1)}, bf16[16,32,128]{2,1...) custom-call(bf16[16,256,128]{2,1,0:T(8,128)(2,1)} %bitcast.15, ...), custom_call_target="tpu_custom_call" | custom-call | tf_op jit(solution)/shard_map/prepare/pallas_call | solution.py:302
  2.3 2.6 %collective-permute-start = (bf16[16,32,128]{2,1,0:T(8,128)(2,1)S(1)}, bf16[16,32,128]{2,1,0:T(8,128)(2,1)S(1)}, u32[]{:S(2)}, u32[]{:S(2)}) collective-permute-start(bf16[16,32,128]{2,1,0:T(8,128)(2,1)S(1)} %get-tuple-element.23), channel_id=1, source_target_pairs={{0,8},{8,16},{16,24},{24,32},{32,40},{40,48},{48,56},{56,0},{1,9},... | collective-permute-start | bytes 393224 | tf_op jit(solution)/shard_map/ppermute | solution.py:255
  4.9 4.3 %collective-permute-start.1 = (bf16[16,32,128]{2,1,0:T(8,128)(2,1)S(1)}, bf16[16,32,128]{2,1,0:T(8,128)(2,1)S(1)}, u32[]{:S(2)}, u32[]{:S(2)}) collective-permute-start(bf16[16,32,128]{2,1,0:T(8,128)(2,1)S(1)} %get-tuple-element.24), channel_id=1, source_target_pairs={{8,0},{16,8},{24,16},{32,24},{40,32},{48,40},{56,48},{0,56},{9,1},... | collective-permute-start | bytes 393224 | tf_op jit(solution)/shard_map/ppermute | solution.py:260
  9.1 1.9 %collective-permute-start.2 = (bf16[2,256,128]{2,1,0:T(8,128)(2,1)S(1)}, bf16[2,256,128]{2,1,0:T(8,128)(2,1)S(1)}, u32[]{:S(2)}, u32[]{:S(2)}) collective-permute-start(bf16[2,256,128]{2,1,0:T(8,128)(2,1)S(1)} %get-tuple-element.25), channel_id=1, source_target_pairs={{0,64},{64,128},{128,192},{192,256},{256,320},{320,384},{384,448},... | collective-permute-start | bytes 393224 | tf_op jit(solution)/shard_map/ppermute | solution.py:255
  11.0 1.9 %collective-permute-start.3 = (bf16[16,32,128]{2,1,0:T(8,128)(2,1)S(1)}, bf16[16,32,128]{2,1,0:T(8,128)(2,1)S(1)}, u32[]{:S(2)}, u32[]{:S(2)}) collective-permute-start(bf16[16,32,128]{2,1,0:T(8,128)(2,1)S(1)} %get-tuple-element.26), channel_id=1, source_target_pairs={{0,1},{1,2},{2,3},{3,4},{4,5},{5,6},{6,7},{7,0},{8,9},{9,10},{10,1... | collective-permute-start | bytes 393224 | tf_op jit(solution)/shard_map/ppermute | solution.py:255
  13.0 4.6 %collective-permute-start.4 = (bf16[2,256,128]{2,1,0:T(8,128)(2,1)S(1)}, bf16[2,256,128]{2,1,0:T(8,128)(2,1)S(1)}, u32[]{:S(2)}, u32[]{:S(2)}) collective-permute-start(bf16[2,256,128]{2,1,0:T(8,128)(2,1)S(1)} %get-tuple-element.27), channel_id=1, source_target_pairs={{64,0},{128,64},{192,128},{256,192},{320,256},{384,320},{448,384},... | collective-permute-start | bytes 393224 | tf_op jit(solution)/shard_map/ppermute | solution.py:260
  17.6 0.0 collective-permute-done.ylo
  17.6 6.9 %collective-permute-start.5 = (bf16[16,32,128]{2,1,0:T(8,128)(2,1)S(1)}, bf16[16,32,128]{2,1,0:T(8,128)(2,1)S(1)}, u32[]{:S(2)}, u32[]{:S(2)}) collective-permute-start(bf16[16,32,128]{2,1,0:T(8,128)(2,1)S(1)} %get-tuple-element.28), channel_id=1, source_target_pairs={{1,0},{2,1},{3,2},{4,3},{5,4},{6,5},{7,6},{0,7},{9,8},{10,9},{11,1... | collective-permute-start | bytes 393224 | tf_op jit(solution)/shard_map/ppermute | solution.py:260
  24.5 1.3 %inner.1 = f32[16,256,128]{2,1,0:T(8,128)S(1)} custom-call(bf16[16,256,128]{2,1,0:T(8,128)(2,1)S(1)} %get-tuple-element.20.p, f32[16,16,16]{2,1,0:T(8,128)S(1)} %get-tuple-element.21.pot, bf16[256,384]{1,0:T(8,128)(2,1)S(1)} %get-tuple-element.22.weights), custom_call_target="tpu_custom_call" | custom-call | tf_op jit(solution)/shard_map/inner/pallas_call | solution.py:321
  25.9 0.0 collective-permute-done.1.yhi
  25.9 0.0 collective-permute-done.2.xlo
  25.9 0.0 collective-permute-done.3.zlo
  25.9 0.0 collective-permute-done.4.xhi
  25.9 0.5 collective-permute-done.5.zhi
  26.4 1.7 %apply.1 = (bf16[16,256,128]{2,1,0:T(8,128)(2,1)S(1)}, bf16[16,256,128]{2,1,0:T(8,128)(2,1)S(1)}, f32[256,128]{1,0:T(8,128)S(1)}) custom-call(bf16[16,256,128]{2,1,0:T(8,128)(2,1)S(1)} %get-tuple-element.20.p, f32[16,256,128]{2,1,0:T(8,128)S(1)} %inner.1, bf16[16,32,128]{2,1,0:T(8,128)(2,1)S(1)} %collective-permute-done.ylo, ...), custom_call_target="tpu_custom_call" | custom-call | tf_op jit(solution)/shard_map/apply/pallas_call | solution.py:324
  28.1 12.8 %all_to_all.15 = f32[32,8,128]{2,1,0:T(8,128)S(1)} all-to-all(f32[32,8,128]{2,1,0:T(8,128)S(1)} %bitcast.14), channel_id=1, replica_groups=mesh['gx_0'=4,'gx_1'=2,'gy_0'=4,'gy_1'=2,'gz_0'=4,'gz_1'=2] {'gy_0','gy_..., dimensions={0} | all-to-all | bytes 262144 | tf_op jit(solution)/shard_map/all_to_all | solution.py:276
  41.0 22.1 %all_to_all.16 = f32[16,8,128]{2,1,0:T(8,128)S(1)} all-to-all(f32[16,8,128]{2,1,0:T(8,128)S(1)} %broadcast_in_dim.6), channel_id=1, replica_groups=mesh['gx_0'=4,'gx_1'=2,'gy_0'=4,'gy_1'=2,'gz_0'=4,'gz_1'=2] {'gx_0','gz_0'}, dimensions={0} | all-to-all | bytes 131072 | tf_op jit(solution)/shard_map/all_to_all | solution.py:276
  63.2 11.8 %all_to_all.17 = f32[32,8,128]{2,1,0:T(8,128)S(1)} all-to-all(f32[32,8,128]{2,1,0:T(8,128)S(1)} %broadcast_in_dim.7), channel_id=1, replica_groups=mesh['gx_0'=4,'gx_1'=2,'gy_0'=4,'gy_1'=2,'gz_0'=4,'gz_1'=2] {'gy_0','gy_..., dimensions={0} | all-to-all | bytes 262144 | tf_op jit(solution)/shard_map/all_to_all | solution.py:276
  75.0 6.8 %finish.1 = (f32[4096,128]{1,0:T(8,128)}, bf16[4096,128]{1,0:T(8,128)(2,1)}, f32[1,128]{1,0:T(1,128)}, f32[1,128]{1,0:T(1,128)}) custom-call(f32[256,128]{1,0:T(8,128)S(1)} %bitcast.13, bf16[4096,128]{1,0:T(8,128)(2,1)S(1)} %bitcast.10, bf16[4096,128]{1,0:T(8,128)(2,1)S(1)} %bitcast.11, bf16[4096,128]{1,0:T(8,128)(2,1)S(1)} %bitcast.12), custom_call_target="tpu_custom_call" | custom-call | tf_op jit(solution)/shard_map/finish/pallas_call | solution.py:334
  (4 shorter events, 0.1 us)
Async XLA Ops:
  2.3 15.3 %collective-permute-start = (bf16[16,32,128]{2,1,0:T(8,128)(2,1)S(1)}, bf16[16,32,128]{2,1,0:T(8,128)(2,1)S(1)}, u32[]{:S(2)}, u32[]{:S(2)}) collective-permute-start(bf16[16,32,128]{2,1,0:T(8,128)(2,1)S(1)} %get-tuple-element.23), channel_id=1, source_target_pairs={{0,8},{8,16},{16,24},{24,32},{32,40},{40,48},{48,56},{56,0},{1,9},... | collective-permute-start | bytes 393224 | tf_op jit(solution)/shard_map/ppermute | solution.py:255
  4.9 21.0 %collective-permute-start.1 = (bf16[16,32,128]{2,1,0:T(8,128)(2,1)S(1)}, bf16[16,32,128]{2,1,0:T(8,128)(2,1)S(1)}, u32[]{:S(2)}, u32[]{:S(2)}) collective-permute-start(bf16[16,32,128]{2,1,0:T(8,128)(2,1)S(1)} %get-tuple-element.24), channel_id=1, source_target_pairs={{8,0},{16,8},{24,16},{32,24},{40,32},{48,40},{56,48},{0,56},{9,1},... | collective-permute-start | bytes 393224 | tf_op jit(solution)/shard_map/ppermute | solution.py:260
  9.1 16.7 %collective-permute-start.2 = (bf16[2,256,128]{2,1,0:T(8,128)(2,1)S(1)}, bf16[2,256,128]{2,1,0:T(8,128)(2,1)S(1)}, u32[]{:S(2)}, u32[]{:S(2)}) collective-permute-start(bf16[2,256,128]{2,1,0:T(8,128)(2,1)S(1)} %get-tuple-element.25), channel_id=1, source_target_pairs={{0,64},{64,128},{128,192},{192,256},{256,320},{320,384},{384,448},... | collective-permute-start | bytes 393224 | tf_op jit(solution)/shard_map/ppermute | solution.py:255
  11.0 14.8 %collective-permute-start.3 = (bf16[16,32,128]{2,1,0:T(8,128)(2,1)S(1)}, bf16[16,32,128]{2,1,0:T(8,128)(2,1)S(1)}, u32[]{:S(2)}, u32[]{:S(2)}) collective-permute-start(bf16[16,32,128]{2,1,0:T(8,128)(2,1)S(1)} %get-tuple-element.26), channel_id=1, source_target_pairs={{0,1},{1,2},{2,3},{3,4},{4,5},{5,6},{6,7},{7,0},{8,9},{9,10},{10,1... | collective-permute-start | bytes 393224 | tf_op jit(solution)/shard_map/ppermute | solution.py:255
  13.0 12.9 %collective-permute-start.4 = (bf16[2,256,128]{2,1,0:T(8,128)(2,1)S(1)}, bf16[2,256,128]{2,1,0:T(8,128)(2,1)S(1)}, u32[]{:S(2)}, u32[]{:S(2)}) collective-permute-start(bf16[2,256,128]{2,1,0:T(8,128)(2,1)S(1)} %get-tuple-element.27), channel_id=1, source_target_pairs={{64,0},{128,64},{192,128},{256,192},{320,256},{384,320},{448,384},... | collective-permute-start | bytes 393224 | tf_op jit(solution)/shard_map/ppermute | solution.py:260
  17.6 8.9 %collective-permute-start.5 = (bf16[16,32,128]{2,1,0:T(8,128)(2,1)S(1)}, bf16[16,32,128]{2,1,0:T(8,128)(2,1)S(1)}, u32[]{:S(2)}, u32[]{:S(2)}) collective-permute-start(bf16[16,32,128]{2,1,0:T(8,128)(2,1)S(1)} %get-tuple-element.28), channel_id=1, source_target_pairs={{1,0},{2,1},{3,2},{4,3},{5,4},{6,5},{7,6},{0,7},{9,8},{10,9},{11,1... | collective-permute-start | bytes 393224 | tf_op jit(solution)/shard_map/ppermute | solution.py:260

commit v5 on v4

--- a/solution.py
+++ b/solution.py
@@ -105,7 +105,7 @@
         slab(x, [step for step in (-2, -1, 1, 2) if 0 <= x + step < cx])
 
 
-def apply_kernel(p, inner, ylo, yhi, xlo, zlo, xhi, zhi, weights, high, low, sums):
+def apply_kernel(p, inner, xlo, xhi, zlo, zhi, ylo, yhi, weights, high, low, sums):
     cx, cells, bands = p.shape
     b = bands
 
@@ -315,9 +315,9 @@
         name="prepare",
     )(*map(far, (planes, potential, weights)))
     xlow, xhigh, ylow, yhigh, zlow, zhigh = edges
+    xlo, xhi = from_below(xhigh, GX), from_above(xlow, GX)
+    zlo, zhi = from_below(zhigh, GZ), from_above(zlow, GZ)
     ylo, yhi = from_below(yhigh, GY), from_above(ylow, GY)
-    xlo, zlo = from_below(xhigh, GX), from_below(zhigh, GZ)
-    xhi, zhi = from_above(xlow, GX), from_above(zlow, GZ)
     inner = kernel_call(
         inner_kernel, (on_chip(shape, jnp.float32),), [on_chip] * 3, [on_chip], name="inner"
     )(*map(near, (p, pot, w)))[0]
@@ -327,7 +327,7 @@
         [on_chip] * 9,
         [on_chip] * 3,
         name="apply",
-    )(*map(near, (p, inner, ylo, yhi, xlo, zlo, xhi, zhi, w)))
+    )(*map(near, (p, inner, xlo, xhi, zlo, zhi, ylo, yhi, w)))
     sums = sum_everywhere(sums)
     flat = (cells, bands)
     line = jax.ShapeDtypeStruct((1, bands), jnp.float32)

time: 82.1 us -> 81.8 us (level)
  blocking collectives: 46.7 us -> 43.4 us
  waiting for transfers between devices: 0.55 us -> 3.02 us
    ppermute x3, starting transfers between devices: 6.43 us -> 10.4 us  [from_below(): lax.ppermute(edge, axes, [(i, (i + 1) % count) for i in range(count)])]
    ppermute x3, starting transfers between devices: 15.8 us -> 12.4 us  [from_above(): lax.ppermute(edge, axes, [((i + 1) % count, i) for i in range(count)])]
    all_to_all x3, blocking collectives: 46.7 us -> 43.4 us  [exchange(): return lax.all_to_all(blocks, axes, split_axis=0, concat_axis=0, tiled=True)]
    ppermute x3, waiting for transfers between devices: 0.54 us -> 2.45 us  [from_above(): lax.ppermute(edge, axes, [((i + 1) % count, i) for i in range(count)])]
  transfers between devices with their start and end apart: 6 -> 6, of which waited for: 1 -> 2; matrix products, arithmetic and copies ran while one was open for 0% -> 0% of each run, Pallas kernels for 2% -> 2%
where the time goes in v5:
time: 81.8 us; the launch traced here: 81.4 us
  blocking collectives  43.4 us (53%)
  starting transfers between devices  22.8 us (28%)
  Pallas kernels  11.5 us (14%)
  waiting for transfers between devices  3.02 us (4%)
    all_to_all x3, blocking collectives, exchange(): return lax.all_to_all(blocks, axes, split_axis=0, concat_axis=0, tiled=True)  43.4 us
    ppermute x3, starting transfers between devices, from_above(): lax.ppermute(edge, axes, [((i + 1) % count, i) for i in range(count)])  12.4 us
    ppermute x3, starting transfers between devices, from_below(): lax.ppermute(edge, axes, [(i, (i + 1) % count) for i in range(count)])  10.4 us
    pallas_call x1, Pallas kernels, local(): kernel_call(functools.partial(finish_kernel, total_cells), (jax.ShapeDtyp...  6.77 us
    ppermute x3, waiting for transfers between devices, from_above(): lax.ppermute(edge, axes, [((i + 1) % count, i) for i in range(count)])  2.45 us
    pallas_call x1, Pallas kernels, local(): kernel_call(apply_kernel, (half(*shape), half(*shape), on_chip((2 * bands...  1.72 us
  transfers between devices with their start and end apart: 6, of which 2 were waited for; matrix products, arithmetic and copies ran while one was open for 0% of the time, Pallas kernels for 2%

profile of v5, /device:TPU:1, one launch (start us, length us, event | category | flops | bytes accessed | tf_op | source)
XLA Modules:
  0.0 81.4 jit_solution(17631849933737912099)
XLA Ops:
  0.6 1.6 %prepare.1 = (bf16[16,256,128]{2,1,0:T(8,128)(2,1)S(1)}, bf16[2,256,128]{2,1,0:T(8,128)(2,1)S(1)}, bf16[2,256,128]{2,1,0:T(8,128)(2,1)S(1)}, bf16[16,32,128]{2,1...) custom-call(bf16[16,256,128]{2,1,0:T(8,128)(2,1)} %bitcast.15, ...), custom_call_target="tpu_custom_call" | custom-call | tf_op jit(solution)/shard_map/prepare/pallas_call | solution.py:302
  2.3 4.0 %collective-permute-start = (bf16[2,256,128]{2,1,0:T(8,128)(2,1)S(1)}, bf16[2,256,128]{2,1,0:T(8,128)(2,1)S(1)}, u32[]{:S(2)}, u32[]{:S(2)}) collective-permute-start(bf16[2,256,128]{2,1,0:T(8,128)(2,1)S(1)} %get-tuple-element.23), channel_id=1, source_target_pairs={{0,64},{64,128},{128,192},{192,256},{256,320},{320,384},{384,448},... | collective-permute-start | bytes 393224 | tf_op jit(solution)/shard_map/ppermute | solution.py:255
  6.3 3.8 %collective-permute-start.1 = (bf16[2,256,128]{2,1,0:T(8,128)(2,1)S(1)}, bf16[2,256,128]{2,1,0:T(8,128)(2,1)S(1)}, u32[]{:S(2)}, u32[]{:S(2)}) collective-permute-start(bf16[2,256,128]{2,1,0:T(8,128)(2,1)S(1)} %get-tuple-element.24), channel_id=1, source_target_pairs={{64,0},{128,64},{192,128},{256,192},{320,256},{384,320},{448,384},... | collective-permute-start | bytes 393224 | tf_op jit(solution)/shard_map/ppermute | solution.py:260
  10.1 4.0 %collective-permute-start.2 = (bf16[16,32,128]{2,1,0:T(8,128)(2,1)S(1)}, bf16[16,32,128]{2,1,0:T(8,128)(2,1)S(1)}, u32[]{:S(2)}, u32[]{:S(2)}) collective-permute-start(bf16[16,32,128]{2,1,0:T(8,128)(2,1)S(1)} %get-tuple-element.25), channel_id=1, source_target_pairs={{0,1},{1,2},{2,3},{3,4},{4,5},{5,6},{6,7},{7,0},{8,9},{9,10},{10,1... | collective-permute-start | bytes 393224 | tf_op jit(solution)/shard_map/ppermute | solution.py:255
  14.1 8.6 %collective-permute-start.3 = (bf16[16,32,128]{2,1,0:T(8,128)(2,1)S(1)}, bf16[16,32,128]{2,1,0:T(8,128)(2,1)S(1)}, u32[]{:S(2)}, u32[]{:S(2)}) collective-permute-start(bf16[16,32,128]{2,1,0:T(8,128)(2,1)S(1)} %get-tuple-element.26), channel_id=1, source_target_pairs={{1,0},{2,1},{3,2},{4,3},{5,4},{6,5},{7,6},{0,7},{9,8},{10,9},{11,1... | collective-permute-start | bytes 393224 | tf_op jit(solution)/shard_map/ppermute | solution.py:260
  22.7 2.3 %collective-permute-start.4 = (bf16[16,32,128]{2,1,0:T(8,128)(2,1)S(1)}, bf16[16,32,128]{2,1,0:T(8,128)(2,1)S(1)}, u32[]{:S(2)}, u32[]{:S(2)}) collective-permute-start(bf16[16,32,128]{2,1,0:T(8,128)(2,1)S(1)} %get-tuple-element.27), channel_id=1, source_target_pairs={{0,8},{8,16},{16,24},{24,32},{32,40},{40,48},{48,56},{56,0},{1,9},... | collective-permute-start | bytes 393224 | tf_op jit(solution)/shard_map/ppermute | solution.py:255
  25.1 0.0 collective-permute-done.xlo
  25.1 0.0 collective-permute-start.5
  25.1 1.3 %inner.1 = f32[16,256,128]{2,1,0:T(8,128)S(1)} custom-call(bf16[16,256,128]{2,1,0:T(8,128)(2,1)S(1)} %get-tuple-element.20.p, f32[16,16,16]{2,1,0:T(8,128)S(1)} %get-tuple-element.21.pot, bf16[256,384]{1,0:T(8,128)(2,1)S(1)} %get-tuple-element.22.weights), custom_call_target="tpu_custom_call" | custom-call | tf_op jit(solution)/shard_map/inner/pallas_call | solution.py:321
  26.4 0.0 collective-permute-done.1.xhi
  26.4 0.0 collective-permute-done.2.zlo
  26.4 0.0 collective-permute-done.3.zhi
  26.4 0.6 collective-permute-done.4.ylo
  27.0 2.4 %collective-permute-done.5.yhi = bf16[16,32,128]{2,1,0:T(8,128)(2,1)S(1)} collective-permute-done((bf16[16,32,128]{2,1,0:T(8,128)(2,1)S(1)}, bf16[16,32,128]{2,1,0:T(8,128)(2,1)S(1)}, u32[]{:S(2)}, u32[]{:S(2)}) %collective-permute-start.5) | collective-permute-done | bytes 131104 | tf_op jit(solution)/shard_map/ppermute | solution.py:260
  29.5 1.7 %apply.1 = (bf16[16,256,128]{2,1,0:T(8,128)(2,1)S(1)}, bf16[16,256,128]{2,1,0:T(8,128)(2,1)S(1)}, f32[256,128]{1,0:T(8,128)S(1)}) custom-call(bf16[16,256,128]{2,1,0:T(8,128)(2,1)S(1)} %get-tuple-element.20.p, f32[16,256,128]{2,1,0:T(8,128)S(1)} %inner.1, bf16[2,256,128]{2,1,0:T(8,128)(2,1)S(1)} %collective-permute-done.xlo, ...), custom_call_target="tpu_custom_call" | custom-call | tf_op jit(solution)/shard_map/apply/pallas_call | solution.py:324
  31.2 11.1 %all_to_all.15 = f32[32,8,128]{2,1,0:T(8,128)S(1)} all-to-all(f32[32,8,128]{2,1,0:T(8,128)S(1)} %bitcast.14), channel_id=1, replica_groups=mesh['gx_0'=4,'gx_1'=2,'gy_0'=4,'gy_1'=2,'gz_0'=4,'gz_1'=2] {'gy_0','gy_..., dimensions={0} | all-to-all | bytes 262144 | tf_op jit(solution)/shard_map/all_to_all | solution.py:276
  42.3 20.5 %all_to_all.16 = f32[16,8,128]{2,1,0:T(8,128)S(1)} all-to-all(f32[16,8,128]{2,1,0:T(8,128)S(1)} %broadcast_in_dim.6), channel_id=1, replica_groups=mesh['gx_0'=4,'gx_1'=2,'gy_0'=4,'gy_1'=2,'gz_0'=4,'gz_1'=2] {'gx_0','gz_0'}, dimensions={0} | all-to-all | bytes 131072 | tf_op jit(solution)/shard_map/all_to_all | solution.py:276
  62.9 11.8 %all_to_all.17 = f32[32,8,128]{2,1,0:T(8,128)S(1)} all-to-all(f32[32,8,128]{2,1,0:T(8,128)S(1)} %broadcast_in_dim.7), channel_id=1, replica_groups=mesh['gx_0'=4,'gx_1'=2,'gy_0'=4,'gy_1'=2,'gz_0'=4,'gz_1'=2] {'gy_0','gy_..., dimensions={0} | all-to-all | bytes 262144 | tf_op jit(solution)/shard_map/all_to_all | solution.py:276
  74.7 6.8 %finish.1 = (f32[4096,128]{1,0:T(8,128)}, bf16[4096,128]{1,0:T(8,128)(2,1)}, f32[1,128]{1,0:T(1,128)}, f32[1,128]{1,0:T(1,128)}) custom-call(f32[256,128]{1,0:T(8,128)S(1)} %bitcast.13, bf16[4096,128]{1,0:T(8,128)(2,1)S(1)} %bitcast.10, bf16[4096,128]{1,0:T(8,128)(2,1)S(1)} %bitcast.11, bf16[4096,128]{1,0:T(8,128)(2,1)S(1)} %bitcast.12), custom_call_target="tpu_custom_call" | custom-call | tf_op jit(solution)/shard_map/finish/pallas_call | solution.py:334
  (4 shorter events, 0.1 us)
Async XLA Ops:
  2.3 22.8 %collective-permute-start = (bf16[2,256,128]{2,1,0:T(8,128)(2,1)S(1)}, bf16[2,256,128]{2,1,0:T(8,128)(2,1)S(1)}, u32[]{:S(2)}, u32[]{:S(2)}) collective-permute-start(bf16[2,256,128]{2,1,0:T(8,128)(2,1)S(1)} %get-tuple-element.23), channel_id=1, source_target_pairs={{0,64},{64,128},{128,192},{192,256},{256,320},{320,384},{384,448},... | collective-permute-start | bytes 393224 | tf_op jit(solution)/shard_map/ppermute | solution.py:255
  6.3 20.1 %collective-permute-start.1 = (bf16[2,256,128]{2,1,0:T(8,128)(2,1)S(1)}, bf16[2,256,128]{2,1,0:T(8,128)(2,1)S(1)}, u32[]{:S(2)}, u32[]{:S(2)}) collective-permute-start(bf16[2,256,128]{2,1,0:T(8,128)(2,1)S(1)} %get-tuple-element.24), channel_id=1, source_target_pairs={{64,0},{128,64},{192,128},{256,192},{320,256},{384,320},{448,384},... | collective-permute-start | bytes 393224 | tf_op jit(solution)/shard_map/ppermute | solution.py:260
  10.1 16.3 %collective-permute-start.2 = (bf16[16,32,128]{2,1,0:T(8,128)(2,1)S(1)}, bf16[16,32,128]{2,1,0:T(8,128)(2,1)S(1)}, u32[]{:S(2)}, u32[]{:S(2)}) collective-permute-start(bf16[16,32,128]{2,1,0:T(8,128)(2,1)S(1)} %get-tuple-element.25), channel_id=1, source_target_pairs={{0,1},{1,2},{2,3},{3,4},{4,5},{5,6},{6,7},{7,0},{8,9},{9,10},{10,1... | collective-permute-start | bytes 393224 | tf_op jit(solution)/shard_map/ppermute | solution.py:255
  14.1 12.3 %collective-permute-start.3 = (bf16[16,32,128]{2,1,0:T(8,128)(2,1)S(1)}, bf16[16,32,128]{2,1,0:T(8,128)(2,1)S(1)}, u32[]{:S(2)}, u32[]{:S(2)}) collective-permute-start(bf16[16,32,128]{2,1,0:T(8,128)(2,1)S(1)} %get-tuple-element.26), channel_id=1, source_target_pairs={{1,0},{2,1},{3,2},{4,3},{5,4},{6,5},{7,6},{0,7},{9,8},{10,9},{11,1... | collective-permute-start | bytes 393224 | tf_op jit(solution)/shard_map/ppermute | solution.py:260
  22.7 4.3 %collective-permute-start.4 = (bf16[16,32,128]{2,1,0:T(8,128)(2,1)S(1)}, bf16[16,32,128]{2,1,0:T(8,128)(2,1)S(1)}, u32[]{:S(2)}, u32[]{:S(2)}) collective-permute-start(bf16[16,32,128]{2,1,0:T(8,128)(2,1)S(1)} %get-tuple-element.27), channel_id=1, source_target_pairs={{0,8},{8,16},{16,24},{24,32},{32,40},{40,48},{48,56},{56,0},{1,9},... | collective-permute-start | bytes 393224 | tf_op jit(solution)/shard_map/ppermute | solution.py:255
  25.1 4.4 %collective-permute-start.5 = (bf16[16,32,128]{2,1,0:T(8,128)(2,1)S(1)}, bf16[16,32,128]{2,1,0:T(8,128)(2,1)S(1)}, u32[]{:S(2)}, u32[]{:S(2)}) collective-permute-start(bf16[16,32,128]{2,1,0:T(8,128)(2,1)S(1)} %get-tuple-element.28), channel_id=1, source_target_pairs={{8,0},{16,8},{24,16},{32,24},{40,32},{48,40},{56,48},{0,56},{9,1},... | collective-permute-start | bytes 393224 | tf_op jit(solution)/shard_map/ppermute | solution.py:260

commit v6 on v5

--- a/solution.py
+++ b/solution.py
@@ -12,8 +12,8 @@
 GX = ("gx_0", "gx_1")
 GY = ("gy_0", "gy_1")
 GZ = ("gz_0", "gz_1")
-NEAR = ("gy_0", "gy_1", "gx_1", "gz_1")
-FAR = ("gx_0", "gz_0")
+NEAR = ("gz_1", "gx_1", "gy_1", "gy_0")
+FAR = ("gz_0", "gx_0")
 HIGHEST = lax.Precision.HIGHEST
 CHUNKS = (512,) * 8
 VMEM_LIMIT = 24 * 2**20
@@ -213,12 +213,17 @@
         w[at, bands:, :bands] = none
         w[at, bands:, bands:] = part if at < 2 else w[0, bands:, bands:]
 
-    def diagonal(matrix):
-        product = jnp.dot(matrix, turned, precision=HIGHEST, preferred_element_type=jnp.float32)
-        return jnp.sum(product * turned, axis=0, keepdims=True)
-
-    quotient = diagonal(cross)
-    squares = diagonal(square) - quotient * quotient * (2.0 - diagonal(gram))
+    product = jnp.dot(
+        jnp.concatenate([cross, square, gram], axis=0),
+        turned,
+        precision=HIGHEST,
+        preferred_element_type=jnp.float32,
+    )
+    quotient, applied_square, rotated_square = (
+        jnp.sum(product[i : i + bands] * turned, axis=0, keepdims=True)
+        for i in range(0, 3 * bands, bands)
+    )
+    squares = applied_square - quotient * quotient * (2.0 - rotated_square)
     quotients[...] = quotient
     norms[...] = jnp.sqrt(jnp.maximum(squares, 0.0) + 1e-06)
     copies = []

time: 81.8 us -> 81.8 us (level)
  no operation moved by 1% of the time
where the time goes in v6:
time: 81.8 us; the launch traced here: 81.4 us
  blocking collectives  43.4 us (53%)
  starting transfers between devices  22.8 us (28%)
  Pallas kernels  11.4 us (14%)
  waiting for transfers between devices  3.02 us (4%)
    all_to_all x3, blocking collectives, exchange(): return lax.all_to_all(blocks, axes, split_axis=0, concat_axis=0, tiled=True)  43.4 us
    ppermute x3, starting transfers between devices, from_above(): lax.ppermute(edge, axes, [((i + 1) % count, i) for i in range(count)])  12.4 us
    ppermute x3, starting transfers between devices, from_below(): lax.ppermute(edge, axes, [(i, (i + 1) % count) for i in range(count)])  10.4 us
    pallas_call x1, Pallas kernels, local(): kernel_call(functools.partial(finish_kernel, total_cells), (jax.ShapeDtyp...  6.74 us
    ppermute x3, waiting for transfers between devices, from_above(): lax.ppermute(edge, axes, [((i + 1) % count, i) for i in range(count)])  2.45 us
    pallas_call x1, Pallas kernels, local(): kernel_call(apply_kernel, (half(*shape), half(*shape), on_chip((2 * bands...  1.72 us
  transfers between devices with their start and end apart: 6, of which 2 were waited for; matrix products, arithmetic and copies ran while one was open for 0% of the time, Pallas kernels for 2%

profile of v6, /device:TPU:1, one launch (start us, length us, event | category | flops | bytes accessed | tf_op | source)
XLA Modules:
  0.0 81.4 jit_solution(1649644120023302711)
XLA Ops:
  0.6 1.6 %prepare.1 = (bf16[16,256,128]{2,1,0:T(8,128)(2,1)S(1)}, bf16[2,256,128]{2,1,0:T(8,128)(2,1)S(1)}, bf16[2,256,128]{2,1,0:T(8,128)(2,1)S(1)}, bf16[16,32,128]{2,1...) custom-call(bf16[16,256,128]{2,1,0:T(8,128)(2,1)} %bitcast.15, ...), custom_call_target="tpu_custom_call" | custom-call | tf_op jit(solution)/shard_map/prepare/pallas_call | solution.py:307
  2.3 4.0 %collective-permute-start = (bf16[2,256,128]{2,1,0:T(8,128)(2,1)S(1)}, bf16[2,256,128]{2,1,0:T(8,128)(2,1)S(1)}, u32[]{:S(2)}, u32[]{:S(2)}) collective-permute-start(bf16[2,256,128]{2,1,0:T(8,128)(2,1)S(1)} %get-tuple-element.23), channel_id=1, source_target_pairs={{0,64},{64,128},{128,192},{192,256},{256,320},{320,384},{384,448},... | collective-permute-start | bytes 393224 | tf_op jit(solution)/shard_map/ppermute | solution.py:260
  6.3 3.8 %collective-permute-start.1 = (bf16[2,256,128]{2,1,0:T(8,128)(2,1)S(1)}, bf16[2,256,128]{2,1,0:T(8,128)(2,1)S(1)}, u32[]{:S(2)}, u32[]{:S(2)}) collective-permute-start(bf16[2,256,128]{2,1,0:T(8,128)(2,1)S(1)} %get-tuple-element.24), channel_id=1, source_target_pairs={{64,0},{128,64},{192,128},{256,192},{320,256},{384,320},{448,384},... | collective-permute-start | bytes 393224 | tf_op jit(solution)/shard_map/ppermute | solution.py:265
  10.1 4.0 %collective-permute-start.2 = (bf16[16,32,128]{2,1,0:T(8,128)(2,1)S(1)}, bf16[16,32,128]{2,1,0:T(8,128)(2,1)S(1)}, u32[]{:S(2)}, u32[]{:S(2)}) collective-permute-start(bf16[16,32,128]{2,1,0:T(8,128)(2,1)S(1)} %get-tuple-element.25), channel_id=1, source_target_pairs={{0,1},{1,2},{2,3},{3,4},{4,5},{5,6},{6,7},{7,0},{8,9},{9,10},{10,1... | collective-permute-start | bytes 393224 | tf_op jit(solution)/shard_map/ppermute | solution.py:260
  14.1 8.6 %collective-permute-start.3 = (bf16[16,32,128]{2,1,0:T(8,128)(2,1)S(1)}, bf16[16,32,128]{2,1,0:T(8,128)(2,1)S(1)}, u32[]{:S(2)}, u32[]{:S(2)}) collective-permute-start(bf16[16,32,128]{2,1,0:T(8,128)(2,1)S(1)} %get-tuple-element.26), channel_id=1, source_target_pairs={{1,0},{2,1},{3,2},{4,3},{5,4},{6,5},{7,6},{0,7},{9,8},{10,9},{11,1... | collective-permute-start | bytes 393224 | tf_op jit(solution)/shard_map/ppermute | solution.py:265
  22.7 2.3 %collective-permute-start.4 = (bf16[16,32,128]{2,1,0:T(8,128)(2,1)S(1)}, bf16[16,32,128]{2,1,0:T(8,128)(2,1)S(1)}, u32[]{:S(2)}, u32[]{:S(2)}) collective-permute-start(bf16[16,32,128]{2,1,0:T(8,128)(2,1)S(1)} %get-tuple-element.27), channel_id=1, source_target_pairs={{0,8},{8,16},{16,24},{24,32},{32,40},{40,48},{48,56},{56,0},{1,9},... | collective-permute-start | bytes 393224 | tf_op jit(solution)/shard_map/ppermute | solution.py:260
  25.1 0.0 collective-permute-done.xlo
  25.1 0.0 collective-permute-start.5
  25.1 1.3 %inner.1 = f32[16,256,128]{2,1,0:T(8,128)S(1)} custom-call(bf16[16,256,128]{2,1,0:T(8,128)(2,1)S(1)} %get-tuple-element.20.p, f32[16,16,16]{2,1,0:T(8,128)S(1)} %get-tuple-element.21.pot, bf16[256,384]{1,0:T(8,128)(2,1)S(1)} %get-tuple-element.22.weights), custom_call_target="tpu_custom_call" | custom-call | tf_op jit(solution)/shard_map/inner/pallas_call | solution.py:326
  26.4 0.0 collective-permute-done.1.xhi
  26.4 0.0 collective-permute-done.2.zlo
  26.4 0.0 collective-permute-done.3.zhi
  26.4 0.6 collective-permute-done.4.ylo
  27.0 2.4 %collective-permute-done.5.yhi = bf16[16,32,128]{2,1,0:T(8,128)(2,1)S(1)} collective-permute-done((bf16[16,32,128]{2,1,0:T(8,128)(2,1)S(1)}, bf16[16,32,128]{2,1,0:T(8,128)(2,1)S(1)}, u32[]{:S(2)}, u32[]{:S(2)}) %collective-permute-start.5) | collective-permute-done | bytes 131104 | tf_op jit(solution)/shard_map/ppermute | solution.py:265
  29.5 1.7 %apply.1 = (bf16[16,256,128]{2,1,0:T(8,128)(2,1)S(1)}, bf16[16,256,128]{2,1,0:T(8,128)(2,1)S(1)}, f32[256,128]{1,0:T(8,128)S(1)}) custom-call(bf16[16,256,128]{2,1,0:T(8,128)(2,1)S(1)} %get-tuple-element.20.p, f32[16,256,128]{2,1,0:T(8,128)S(1)} %inner.1, bf16[2,256,128]{2,1,0:T(8,128)(2,1)S(1)} %collective-permute-done.xlo, ...), custom_call_target="tpu_custom_call" | custom-call | tf_op jit(solution)/shard_map/apply/pallas_call | solution.py:329
  31.2 11.3 %all_to_all.15 = f32[32,8,128]{2,1,0:T(8,128)S(1)} all-to-all(f32[32,8,128]{2,1,0:T(8,128)S(1)} %bitcast.14), channel_id=1, replica_groups=mesh['gx_0'=4,'gx_1'=2,'gy_0'=4,'gy_1'=2,'gz_0'=4,'gz_1'=2] {'gz_1','gx_..., dimensions={0} | all-to-all | bytes 262144 | tf_op jit(solution)/shard_map/all_to_all | solution.py:281
  42.5 20.4 %all_to_all.16 = f32[16,8,128]{2,1,0:T(8,128)S(1)} all-to-all(f32[16,8,128]{2,1,0:T(8,128)S(1)} %broadcast_in_dim.6), channel_id=1, replica_groups=mesh['gx_0'=4,'gx_1'=2,'gy_0'=4,'gy_1'=2,'gz_0'=4,'gz_1'=2] {'gz_0','gx_0'}, dimensions={0} | all-to-all | bytes 131072 | tf_op jit(solution)/shard_map/all_to_all | solution.py:281
  63.0 11.7 %all_to_all.17 = f32[32,8,128]{2,1,0:T(8,128)S(1)} all-to-all(f32[32,8,128]{2,1,0:T(8,128)S(1)} %broadcast_in_dim.7), channel_id=1, replica_groups=mesh['gx_0'=4,'gx_1'=2,'gy_0'=4,'gy_1'=2,'gz_0'=4,'gz_1'=2] {'gz_1','gx_..., dimensions={0} | all-to-all | bytes 262144 | tf_op jit(solution)/shard_map/all_to_all | solution.py:281
  74.7 6.7 %finish.1 = (f32[4096,128]{1,0:T(8,128)}, bf16[4096,128]{1,0:T(8,128)(2,1)}, f32[1,128]{1,0:T(1,128)}, f32[1,128]{1,0:T(1,128)}) custom-call(f32[256,128]{1,0:T(8,128)S(1)} %bitcast.13, bf16[4096,128]{1,0:T(8,128)(2,1)S(1)} %bitcast.10, bf16[4096,128]{1,0:T(8,128)(2,1)S(1)} %bitcast.11, bf16[4096,128]{1,0:T(8,128)(2,1)S(1)} %bitcast.12), custom_call_target="tpu_custom_call" | custom-call | tf_op jit(solution)/shard_map/finish/pallas_call | solution.py:339
  (4 shorter events, 0.1 us)
Async XLA Ops:
  2.3 22.8 %collective-permute-start = (bf16[2,256,128]{2,1,0:T(8,128)(2,1)S(1)}, bf16[2,256,128]{2,1,0:T(8,128)(2,1)S(1)}, u32[]{:S(2)}, u32[]{:S(2)}) collective-permute-start(bf16[2,256,128]{2,1,0:T(8,128)(2,1)S(1)} %get-tuple-element.23), channel_id=1, source_target_pairs={{0,64},{64,128},{128,192},{192,256},{256,320},{320,384},{384,448},... | collective-permute-start | bytes 393224 | tf_op jit(solution)/shard_map/ppermute | solution.py:260
  6.3 20.1 %collective-permute-start.1 = (bf16[2,256,128]{2,1,0:T(8,128)(2,1)S(1)}, bf16[2,256,128]{2,1,0:T(8,128)(2,1)S(1)}, u32[]{:S(2)}, u32[]{:S(2)}) collective-permute-start(bf16[2,256,128]{2,1,0:T(8,128)(2,1)S(1)} %get-tuple-element.24), channel_id=1, source_target_pairs={{64,0},{128,64},{192,128},{256,192},{320,256},{384,320},{448,384},... | collective-permute-start | bytes 393224 | tf_op jit(solution)/shard_map/ppermute | solution.py:265
  10.1 16.3 %collective-permute-start.2 = (bf16[16,32,128]{2,1,0:T(8,128)(2,1)S(1)}, bf16[16,32,128]{2,1,0:T(8,128)(2,1)S(1)}, u32[]{:S(2)}, u32[]{:S(2)}) collective-permute-start(bf16[16,32,128]{2,1,0:T(8,128)(2,1)S(1)} %get-tuple-element.25), channel_id=1, source_target_pairs={{0,1},{1,2},{2,3},{3,4},{4,5},{5,6},{6,7},{7,0},{8,9},{9,10},{10,1... | collective-permute-start | bytes 393224 | tf_op jit(solution)/shard_map/ppermute | solution.py:260
  14.1 12.3 %collective-permute-start.3 = (bf16[16,32,128]{2,1,0:T(8,128)(2,1)S(1)}, bf16[16,32,128]{2,1,0:T(8,128)(2,1)S(1)}, u32[]{:S(2)}, u32[]{:S(2)}) collective-permute-start(bf16[16,32,128]{2,1,0:T(8,128)(2,1)S(1)} %get-tuple-element.26), channel_id=1, source_target_pairs={{1,0},{2,1},{3,2},{4,3},{5,4},{6,5},{7,6},{0,7},{9,8},{10,9},{11,1... | collective-permute-start | bytes 393224 | tf_op jit(solution)/shard_map/ppermute | solution.py:265
  22.7 4.3 %collective-permute-start.4 = (bf16[16,32,128]{2,1,0:T(8,128)(2,1)S(1)}, bf16[16,32,128]{2,1,0:T(8,128)(2,1)S(1)}, u32[]{:S(2)}, u32[]{:S(2)}) collective-permute-start(bf16[16,32,128]{2,1,0:T(8,128)(2,1)S(1)} %get-tuple-element.27), channel_id=1, source_target_pairs={{0,8},{8,16},{16,24},{24,32},{32,40},{40,48},{48,56},{56,0},{1,9},... | collective-permute-start | bytes 393224 | tf_op jit(solution)/shard_map/ppermute | solution.py:260
  25.1 4.4 %collective-permute-start.5 = (bf16[16,32,128]{2,1,0:T(8,128)(2,1)S(1)}, bf16[16,32,128]{2,1,0:T(8,128)(2,1)S(1)}, u32[]{:S(2)}, u32[]{:S(2)}) collective-permute-start(bf16[16,32,128]{2,1,0:T(8,128)(2,1)S(1)} %get-tuple-element.28), channel_id=1, source_target_pairs={{8,0},{16,8},{24,16},{32,24},{40,32},{48,40},{56,48},{0,56},{9,1},... | collective-permute-start | bytes 393224 | tf_op jit(solution)/shard_map/ppermute | solution.py:265
